TPU v7x, 32 devices: a whole 2x2x4 slice. The times are simulated.
32 devices in a mesh: samp: 32 (over z, y, x, core).
Axes of the slice: x: 2, y: 2, z: 4, core: 2. Of those that a mesh axis runs over, the one named last changes fastest.
Arguments:
- inputs: float32 [30, 65536], P(None, 'samp'), may hold values from -1 to 1
- response: float32 [32, 65536], P(None, 'samp')
- multi_index: int32 [5456, 30], replicated, may hold values from 0 to 3, as said below
- chosen: int32 [3], replicated, may hold values from 0 to 5455, as said below
Outputs:
- residual: float32 [32, 65536], P(None, 'samp')
- correlations: float32 [3, 32, 5456], replicated
- coefficients: float32 [3, 32], replicated
Inputs may be any that keep to these rules, and one draw needn't show every extreme that they name: `multi_index`: rows are distinct; each row's degrees sum to 3 or less. `chosen`: distinct indices.
All inputs are finite; a program needn't handle non-finite values. Where the computation divides by a largest or mean magnitude, that divisor is 1e-20 or more.
Results may differ from a plain program's by a relative error of at most 0.0062.
Values sent between devices are 32-bit elements; how exact they have to be, the bound alone decides.
A program may use at most 128 MiB of HBM per device.

v0:
```python
import functools
import math

import jax
import jax.numpy as jnp
from jax import lax
from jax.experimental import pallas as pl
from jax.experimental.pallas import tpu as pltpu
from jax.sharding import PartitionSpec as P

TILE = 512
NT = (((1,), (1,)), ((), ()))


def up(n, m):
    return -(-n // m) * m


def slots(multi, stride):
    degree = multi.astype(jnp.float32)
    var = lax.broadcasted_iota(jnp.int32, multi.shape, 1).astype(jnp.float32)
    positive = degree > 0.0
    code = degree * float(stride) + var
    count = jnp.sum(jnp.where(positive, 1.0, 0.0), axis=1, keepdims=True)
    total = jnp.sum(jnp.where(positive, code, 0.0), axis=1, keepdims=True)
    high = jnp.max(jnp.where(positive, code, 0.0), axis=1, keepdims=True)
    low = jnp.min(jnp.where(positive, code, 1e6), axis=1, keepdims=True)
    low = jnp.where(count > 0.5, low, 0.0)
    second = jnp.where(count > 1.5, high, 0.0)
    third = jnp.where(count > 2.5, total - low - high, 0.0)
    return low, second, third


def picks(multi, stride):
    levels = 4 * stride
    column = lax.broadcasted_iota(jnp.int32, (multi.shape[0], 2 * levels), 1)
    column = jnp.where(column >= levels, column - levels, column).astype(jnp.float32)
    return jnp.concatenate(
        [jnp.where(column == s, 1.0, 0.0) for s in slots(multi, stride)], axis=0
    ).astype(jnp.bfloat16)


def product(onehot, table):
    rows = onehot.shape[0] // 3
    f = jnp.dot(onehot, table, preferred_element_type=jnp.float32)
    return (f[:rows] * f[rows : 2 * rows] * f[2 * rows :]).astype(jnp.bfloat16)


def split(x):
    high = x.astype(jnp.bfloat16)
    return high, (x - high.astype(jnp.float32)).astype(jnp.bfloat16)


def correlate(cands, stride, chunk, x_ref, res_ref, few_ref, multi_ref, out_ref, active_ref, table, rows):
    step = pl.program_id(0)
    resp, width = res_ref.shape
    levels = 4 * stride
    chunks = [slice(i, i + chunk) for i in range(0, width, chunk)]

    @pl.when(step == 0)
    def _():
        x = x_ref[...]
        second = (3.0 * x * x - 1.0) * 0.5
        third = (5.0 * x * x * x - 3.0 * x) * 0.5
        values = [jnp.ones_like(x), x * math.sqrt(3.0), second * math.sqrt(5.0), third * math.sqrt(7.0)]
        for d, value in enumerate(values):
            high, low = split(value)
            table[d * stride : (d + 1) * stride, :] = high
            table[levels + d * stride : levels + (d + 1) * stride, :] = low
        high, low = split(res_ref[...])
        rows[0:resp, :] = high
        rows[resp : 2 * resp, :] = low
        onehot = picks(few_ref[...], stride)
        for c in chunks:
            active = product(onehot, table[:, c])
            rows[2 * resp :, c] = active
            active_ref[:, c] = active

    onehot = picks(multi_ref[...], stride)
    acc = jnp.zeros((multi_ref.shape[0], rows.shape[0]), jnp.float32)
    for c in chunks:
        psi = product(onehot, table[:, c])
        acc += lax.dot_general(psi, rows[:, c], NT, preferred_element_type=jnp.float32)
    turned = acc.T
    out_ref[0:resp, :] = turned[0:resp] + turned[resp : 2 * resp]
    out_ref[resp:, :] = turned[2 * resp : 2 * resp + out_ref.shape[0] - resp]

    @pl.when(step == pl.num_programs(0) - 1)
    def _():
        res = res_ref[...]
        sq = jnp.sum(res * res, axis=1, keepdims=True)
        tail = out_ref[0:resp, TILE - 128 :]
        lane = lax.broadcasted_iota(jnp.int32, tail.shape, 1)
        out_ref[0:resp, TILE - 128 :] = jnp.where(lane == 127, sq, tail)


def finish(cands, samples, iters, chosen_ref, total_ref, res_ref, active_ref, out_ref, corr_ref, coef_ref):
    resp = res_ref.shape[0]
    total = total_ref[...]
    column = lax.broadcasted_iota(jnp.int32, total.shape, 1)
    picked = [
        jnp.sum(jnp.where(column == chosen_ref[i], total, 0.0), axis=1, keepdims=True)
        for i in range(iters)
    ]
    target = [p[0:resp] for p in picked]
    gram = [[picked[j][resp + i : resp + i + 1] for j in range(iters)] for i in range(iters)]
    sq = total[0:resp, total.shape[1] - 1 :]
    tri = [[None] * iters for _ in range(iters)]
    for i in range(iters):
        for j in range(i + 1):
            s = gram[i][j]
            for m in range(j):
                s = s - tri[i][m] * tri[j][m]
            tri[i][j] = jnp.sqrt(s) if i == j else s / tri[j][j]
    corr = total[0:resp, 0:cands]
    rows = [total[resp + i : resp + i + 1, 0:cands] for i in range(iters)]
    coef = [jnp.zeros((resp, 1), jnp.float32) for _ in range(iters)]
    for k in range(iters):
        norm = math.sqrt(samples) * jnp.sqrt(sq / samples + 1e-06)
        corr_ref[k] = corr * (1.0 / norm)
        largest = jnp.max(jnp.abs(corr), axis=1, keepdims=True)
        gamma = jnp.abs(target[k]) / (largest + 1e-06)
        w = []
        for i in range(k + 1):
            s = target[i]
            for m in range(i):
                s = s - tri[i][m] * w[m]
            w.append(s / tri[i][i])
        for i in reversed(range(k + 1)):
            s = w[i]
            for m in range(i + 1, k + 1):
                s = s - tri[m][i] * w[m]
            w[i] = s / tri[i][i]
        step = [gamma * wi for wi in w]
        for i in range(k + 1):
            coef[i] = coef[i] + step[i]
        if k < iters - 1:
            gain = sum(wi * t for wi, t in zip(w, target))
            sq = jnp.maximum(sq - gamma * (2.0 - gamma) * gain, 0.0)
            target = [
                target[j] - sum(step[i] * gram[i][j] for i in range(k + 1)) for j in range(iters)
            ]
            for i in range(k + 1):
                corr = corr - step[i] * rows[i]
    res = res_ref[...]
    active = active_ref[...].astype(jnp.float32)
    for i in range(iters):
        res = res - coef[i] * active[i : i + 1]
    out_ref[...] = res
    shape = (resp, resp)
    eye = lax.broadcasted_iota(jnp.int32, shape, 0) == lax.broadcasted_iota(jnp.int32, shape, 1)
    lines = [jnp.sum(jnp.where(eye, c, 0.0), axis=0, keepdims=True) for c in coef]
    line = lax.broadcasted_iota(jnp.int32, coef_ref.shape, 0)
    coef_ref[...] = sum(jnp.where(line == i, lines[i], 0.0) for i in range(iters))


def on_device(inputs, response, multi_index, chosen):
    nvars, width = inputs.shape
    samples = width * lax.axis_size("samp")
    cands = multi_index.shape[0]
    iters = chosen.shape[0]
    resp = response.shape[0]
    stride = up(nvars, 16)
    few = up(iters, 16)
    extra = up(iters, 8)
    padded = up(cands + 1, TILE)
    chunk = math.gcd(width, 256)
    x = jnp.pad(inputs, ((0, stride - nvars), (0, 0)))
    picked = jnp.pad(multi_index[chosen], ((0, few - iters), (0, 0)))
    whole = lambda shape: pl.BlockSpec(shape, lambda i: (0, 0))
    local, active = pl.pallas_call(
        functools.partial(correlate, cands, stride, chunk),
        grid=(padded // TILE,),
        in_specs=[
            whole((stride, width)),
            whole((resp, width)),
            whole((few, nvars)),
            pl.BlockSpec((TILE, nvars), lambda i: (i, 0)),
        ],
        out_specs=[pl.BlockSpec((resp + extra, TILE), lambda i: (0, i)), whole((few, width))],
        out_shape=[
            jax.ShapeDtypeStruct((resp + extra, padded), jnp.float32),
            jax.ShapeDtypeStruct((few, width), jnp.bfloat16),
        ],
        scratch_shapes=[
            pltpu.VMEM((8 * stride, width), jnp.bfloat16),
            pltpu.VMEM((2 * resp + few, width), jnp.bfloat16),
        ],
        compiler_params=pltpu.CompilerParams(
            dimension_semantics=("arbitrary",), vmem_limit_bytes=48 * 2**20
        ),
        name="correlate",
    )(x, response, picked, jnp.pad(multi_index, ((0, padded - cands), (0, 0))))
    total = lax.psum(local, "samp")
    vmem = pl.BlockSpec(memory_space=pltpu.VMEM)
    residual, corr, coef = pl.pallas_call(
        functools.partial(finish, cands, samples, iters),
        in_specs=[pl.BlockSpec(memory_space=pltpu.SMEM), vmem, vmem, vmem],
        out_specs=[vmem, vmem, vmem],
        out_shape=[
            jax.ShapeDtypeStruct((resp, width), jnp.float32),
            jax.ShapeDtypeStruct((iters, resp, cands), jnp.float32),
            jax.ShapeDtypeStruct((extra, resp), jnp.float32),
        ],
        compiler_params=pltpu.CompilerParams(vmem_limit_bytes=48 * 2**20),
        name="finish",
    )(chosen, total, response, active)
    return residual, corr, coef[:iters]


def solution(mesh):
    placed = (P(None, "samp"), P(None, "samp"), P(), P())
    return jax.shard_map(
        on_device,
        mesh=mesh,
        in_specs=placed,
        out_specs=(P(None, "samp"), P(), P()),
        check_vma=False,
    )
```

profile of v0, /device:TPU:0, one launch (start us, length us, event | category | flops | bytes accessed | tf_op | source)
XLA Modules:
  0.0 193.7 jit_solution(8946656857403624955)
XLA Ops:
  7.2 0.0 copy-start.3
  7.2 0.0 all-reduce.5.cloned.1.call-start
  7.2 3.0 %copy.7 = s32[5456,30]{1,0:T(8,128)} copy(s32[5456,30]{0,1:T(8,128)} %param.6) | data formatting | bytes 1309440 | tf_op args[2]
  10.2 0.0 copy-done.3
  10.3 0.0 copy-start.4
  10.3 0.0 copy-start
  10.3 2.0 %pad.14.multi_ref = s32[5632,30]{1,0:T(8,128)S(1)} pad(s32[5456,30]{1,0:T(8,128)} %copy.7, s32[]{:T(128)} %constant.2.clone.1), padding=0_176x0_0 | pad | bytes 1330564 | tf_op jit(solution)/shard_map/jit(_pad)/pad | solution.py:193
  12.3 2.3 %gather_fusion = s32[3,30]{1,0:T(4,128)S(1)} fusion(s32[5456,30]{1,0:T(8,128)} %copy.7, s32[1024]{0:T(1024)S(1)} %pad_clamp_fusion), kind=kCustom, calls=%fused_computation | custom fusion | bytes 732 | tf_op jit(solution)/shard_map/gather | solution.py:169
  14.7 0.0 copy-done.4
  14.7 0.0 copy-done
  14.7 33.5 %correlate.1 = (f32[40,5632]{1,0:T(8,128)S(1)}, bf16[16,2048]{1,0:T(8,128)(2,1)S(1)}) custom-call(f32[32,2048]{1,0:T(8,128)S(1)} %pad.12.x_ref, f32[32,2048]{1,0:T(8,128)S(1)} %copy-done, s32[16,30]{1,0:T(8,128)S(1)} %pad.13.few_ref, s32[5632,30]{1,0:T(8,128)S(1)} %pad.14.multi_ref), custom_call_target="tpu_custom_call" | custom-call | tf_op jit(solution)/shard_map/correlate/pallas_call | solution.py:171
  48.2 0.0 copy-start.2
  48.2 0.9 copy-done.2
  49.1 0.0 all-reduce.5.cloned.1.call-update
  49.1 133.0 %all-reduce.5.cloned.1.call-done.total_ref = f32[40,5632]{1,0:T(8,128)} async-done(((f32[40,5632]{1,0:T(8,128)}), f32[40,5632]{1,0:T(8,128)}) %all-reduce.5.cloned.1.call-update) | async-done | bytes 901136 | tf_op jit(solution)/shard_map/psum | solution.py:194
  182.2 0.0 copy-start.1
  182.2 1.2 copy-done.1
  183.4 2.9 %finish.1 = (f32[32,2048]{1,0:T(8,128)}, f32[3,32,5456]{2,1,0:T(8,128)}, f32[8,32]{1,0:T(8,128)S(1)}) custom-call(s32[3]{0:T(128)S(1)} %copy-done.3, f32[40,5632]{1,0:T(8,128)S(1)} %copy-done.1, f32[32,2048]{1,0:T(8,128)S(1)} %copy-done, bf16[16,2048]{1,0:T(8,128)(2,1)S(1)} %get-tuple-element.9.active_ref), custom_call_target="tpu_custom_call" | custom-call | tf_op jit(solution)/shard_map/finish/pallas_call | solution.py:196
  186.3 0.6 slice.3
  (4 shorter events, 0.0 us)
Async XLA Ops:
  7.2 3.1 %copy-start.3 = (s32[3]{0:T(128)S(1)}, s32[3]{0:T(128)}, u32[]{:S(2)}) copy-start(s32[3]{0:T(128)} %chosen_ref.1) | copy-start | bytes 40
  7.2 175.0 %all-reduce.5.cloned.1.call-start = ((), (), s32[]{:S(2)}) async-start(), calls=%async_computation | async-start | bytes 1802240 | tf_op jit(solution)/shard_map/psum | solution.py:194
  10.3 4.4 %copy-start.4 = (f32[30,2048]{1,0:T(8,128)S(1)}, f32[30,2048]{1,0:T(8,128)}, u32[]{:S(2)}) copy-start(f32[30,2048]{1,0:T(8,128)} %param.4) | copy-start | bytes 737284
  10.3 4.4 %copy-start = (f32[32,2048]{1,0:T(8,128)S(1)}, f32[32,2048]{1,0:T(8,128)}, u32[]{:S(2)}) copy-start(f32[32,2048]{1,0:T(8,128)} %res_ref.3) | copy-start | bytes 786436
  48.2 0.9 copy-start.2
  182.2 1.2 copy-start.1
Sparse Core Ops, SparseCore 0:
  49.3 132.8 all-reduce.4
where the time goes:
time: 194 us
  waiting for transfers between devices  133 us (69%)
  Pallas kernels  36.4 us (19%)
  between operations  14.1 us (7%)
  local copies, waits for them, and re-layouts  10.1 us (5%)
    psum x1, waiting for transfers between devices, on_device(): total = lax.psum(local, 'samp')  133 us
    pallas_call x1, Pallas kernels, on_device(): pl.pallas_call(functools.partial(correlate, cands, stride, chunk), grid=(...  33.5 us
    unnamed x11, local copies, waits for them, and re-layouts  5.12 us
  transfers between devices with their start and end apart: 1, of which 1 were waited for; matrix products, arithmetic and copies ran while one was open for 0% of the time, Pallas kernels for 0%

commit v1 on v0

v1 whole, which is shorter than its diff:
```python
import functools
import math

import jax
import jax.numpy as jnp
from jax import lax
from jax.experimental import pallas as pl
from jax.experimental.pallas import tpu as pltpu
from jax.sharding import PartitionSpec as P

LANES = 128
NT = (((1,), (1,)), ((), ()))
TN = (((0,), (0,)), ((), ()))
MESH = pl.DeviceIdType.MESH
VMEM_LIMIT = 56 * 2**20


def up(n, m):
    return -(-n // m) * m


def split(x):
    high = x.astype(jnp.bfloat16)
    return high, (x - high.astype(jnp.float32)).astype(jnp.bfloat16)


class Basis:
    def __init__(self, nvars):
        self.nvars = nvars
        self.stride = up(nvars + 1, 16)
        gaps = []
        d = 1
        while nvars - 3 * d > 0:
            gaps += [(d, e) for e in range(d, nvars - 2 * d)]
            d += 1
        if nvars % 3 == 0:
            gaps.append((nvars // 3, nvars // 3))
        self.triples = len(gaps)
        self.pairs = nvars // 2
        self.squares = nvars - 1
        self.blocks = [("triple", d, d + e) for d, e in gaps]
        self.blocks += [("pair", d, 0) for d in range(1, self.pairs + 1)]
        self.blocks += [("square", d, 0) for d in range(1, self.squares + 1)]
        self.blocks += [("single", e, 0) for e in range(3)]
        while len(self.blocks) * self.stride % LANES:
            self.blocks.append(("single", 0, 0))
        self.lines = len(self.blocks) * self.stride // LANES
        self.height = up(self.lines + 1, 24)


def place(multi, basis):
    n = float(basis.nvars)
    deg = multi.astype(jnp.float32)
    var = lax.broadcasted_iota(jnp.int32, multi.shape, 0).astype(jnp.float32)
    pos = deg > 0.0
    down = lambda f, x: f(x, axis=0, keepdims=True)
    count = down(jnp.sum, jnp.where(pos, 1.0, 0.0))
    total = down(jnp.sum, jnp.where(pos, var, 0.0))
    low = down(jnp.min, jnp.where(pos, var, n))
    high = down(jnp.max, jnp.where(pos, var, 0.0))
    most = down(jnp.max, deg)
    two = down(jnp.sum, jnp.where(deg > 1.5, var, 0.0))
    mid = total - low - high
    g1, g2 = mid - low, high - mid
    g3 = n - g1 - g2
    at_mid = jnp.logical_and(g2 <= g3, g2 < g1)
    at_high = jnp.logical_and(g3 <= g1, g3 < g2)
    pick = lambda a, b, c: jnp.where(at_high, c, jnp.where(at_mid, b, a))
    d1, d2, start3 = pick(g1, g2, g3), pick(g2, g3, g1), pick(low, mid, high)
    block3 = n * (d1 - 1.0) - 1.5 * d1 * (d1 - 1.0) + d2 - d1
    gap = high - low
    near = gap <= n - gap
    block2 = float(basis.triples - 1) + jnp.where(near, gap, n - gap)
    start2 = jnp.where(near, low, high)
    one = total - two
    turn = two - one
    block21 = float(basis.triples + basis.pairs - 1) + jnp.where(turn > 0.0, turn, turn + n)
    base = float(basis.triples + basis.pairs + basis.squares)
    block1 = base + jnp.maximum(most - 1.0, 0.0)
    squared = most > 1.5
    block = jnp.where(
        count > 2.5, block3, jnp.where(count > 1.5, jnp.where(squared, block21, block2), block1)
    )
    start = jnp.where(
        count > 2.5, start3, jnp.where(count > 1.5, jnp.where(squared, one, start2), low)
    )
    index = block * float(basis.stride) + start
    line = jnp.floor(index * (1.0 / LANES))
    return line, index - line * float(LANES)


def correlate(basis, iters, deep, chosen_ref, x_ref, res_ref, multi_ref, out_ref, active_ref, twice, turned, rows, acc):
    nvars, width = x_ref.shape
    resp = res_ref.shape[0]
    stride = basis.stride
    few = active_ref.shape[0]
    x = x_ref[...]
    second = (3.0 * x * x - 1.0) * 0.5
    third = (5.0 * x * x * x - 3.0 * x) * 0.5
    values = [x * math.sqrt(3.0), second * math.sqrt(5.0), third * math.sqrt(7.0)]
    tall = twice.shape[0] // 3
    for e, value in enumerate(values):
        twice[e * tall : (e + 1) * tall, :] = jnp.ones((tall, width), jnp.float32)
        twice[e * tall : e * tall + nvars, :] = value
    for d in range(nvars):
        if d:
            turned[d * stride : d * stride + nvars - d, :] = values[0][d:]
            turned[d * stride + nvars - d : d * stride + nvars, :] = values[0][:d]
            turned[(nvars + d) * stride : (nvars + d) * stride + nvars - d, :] = values[1][d:]
            turned[(nvars + d) * stride + nvars - d : (nvars + d) * stride + nvars, :] = values[1][:d]
    zero = jnp.zeros((stride - nvars, width), jnp.float32)
    for d in range(1, nvars):
        turned[d * stride + nvars : (d + 1) * stride, :] = zero
        turned[(nvars + d) * stride + nvars : (nvars + d + 1) * stride, :] = zero

    high, low = split(res_ref[...])
    rows[0:resp, :] = high
    rows[resp : 2 * resp, :] = low
    multi = multi_ref[...]
    column = lax.broadcasted_iota(jnp.int32, multi.shape, 1)
    line = lax.broadcasted_iota(jnp.int32, (few, width), 0)
    actives = jnp.zeros((few, width), jnp.float32)
    for k in range(iters):
        deg = jnp.sum(
            jnp.where(column == chosen_ref[k], multi, 0).astype(jnp.float32), axis=1, keepdims=True
        )
        v = jnp.where(
            deg > 2.5,
            values[2],
            jnp.where(deg > 1.5, values[1], jnp.where(deg > 0.5, values[0], 1.0)),
        )
        p = v[0:8]
        for i in range(8, nvars - 7, 8):
            p = p * v[i : i + 8]
        row = p[0:1]
        for i in range(1, min(8, nvars)):
            row = row * p[i : i + 1]
        for i in range(nvars // 8 * 8, nvars):
            row = row * v[i : i + 1]
        actives = jnp.where(line == k, row, actives)
    actives = actives.astype(jnp.bfloat16)
    active_ref[...] = actives
    rows[2 * resp : 2 * resp + few, :] = actives
    rest = rows.shape[0] - 2 * resp - few
    rows[2 * resp + few :, :] = jnp.zeros((rest, width), jnp.bfloat16)

    per = 512 // stride
    groups = [basis.blocks[i : i + per] for i in range(0, len(basis.blocks), per)]

    def step(k, first):
        for g, group in enumerate(groups):
            total = None
            for half in range(0, deep, 256):
                cols = pl.ds(pl.multiple_of(k * deep + half, 256), 256)
                f1 = twice[0:stride, cols]
                parts = []
                held = None
                for kind, d, e in group:
                    if kind == "triple":
                        if held != d:
                            pair = f1 * turned[d * stride : (d + 1) * stride, cols]
                            held = d
                        part = pair * turned[e * stride : (e + 1) * stride, cols]
                    elif kind == "pair":
                        part = f1 * turned[d * stride : (d + 1) * stride, cols]
                    elif kind == "square":
                        part = f1 * turned[(nvars + d) * stride : (nvars + d + 1) * stride, cols]
                    else:
                        part = twice[d * tall : d * tall + stride, cols]
                    parts.append(part.astype(jnp.bfloat16))
                psi = jnp.concatenate(parts, axis=0)
                term = lax.dot_general(psi, rows[:, cols], NT, preferred_element_type=jnp.float32)
                total = term if total is None else total + term
            span = slice(g * per * stride, (g * per + len(group)) * stride)
            acc[span, :] = total if first else acc[span, :] + total

    step(0, True)

    @pl.loop(1, width // deep)
    def _(k):
        step(k, False)

    height = basis.height
    for b in range(basis.lines):
        t = acc[b * LANES : (b + 1) * LANES, :].T
        corr = t[0:resp] + t[resp : 2 * resp]
        for q in range(0, resp, 8):
            out_ref[pl.ds(q * height + b, 8, stride=height), :] = corr[q : q + 8]
        out_ref[pl.ds(resp * height + b, 8, stride=height), :] = t[2 * resp : 2 * resp + 8]
    res = res_ref[...]
    sq = jnp.broadcast_to(jnp.sum(res * res, axis=1, keepdims=True), (resp, LANES))
    for b in range(basis.lines, height):
        for q in range(0, resp, 8):
            out_ref[pl.ds(q * height + b, 8, stride=height), :] = sq[q : q + 8]
        out_ref[pl.ds(resp * height + b, 8, stride=height), :] = jnp.zeros((8, LANES), jnp.float32)


def radices(n):
    result, stride = [], 1
    while n > 1:
        r = 2 if stride == 1 or n == 2 else 4
        if n % r:
            raise ValueError("device count")
        result.append((r, stride))
        stride *= r
        n //= r
    return result


def halving(count, stages):
    plan = []
    for r, _ in stages:
        cut = count % r == 0
        count = count // r if cut else count
        plan.append((cut, count))
    return plan


class Semaphores:
    def __init__(self, send, recv):
        self.send, self.recv, self.used, self.sent = send, recv, 0, []

    def copy(self, src, dst, peer):
        c = pltpu.make_async_remote_copy(
            src_ref=src,
            dst_ref=dst,
            send_sem=self.send.at[self.used],
            recv_sem=self.recv.at[self.used],
            device_id=(peer,),
            device_id_type=MESH,
        )
        self.used += 1
        self.sent.append(c)
        c.start()
        return c


class Stream:
    def __init__(self, ctx, part, lines, offset, held, landed):
        self.ctx, self.lines = ctx, lines
        self.now = (part, offset)
        self.held, self.landed = held, landed
        self.plan = halving(ctx["counts"][id(part)], ctx["stages"])
        self.waiting = None

    def send(self, s):
        r, stride = self.ctx["stages"][s]
        digit = self.ctx["digits"][s]
        cut, count = self.plan[s]
        src, base = self.now
        copies = []
        for j in range(1, r):
            other = lax.rem(digit + j, r)
            peer = self.ctx["me"] + (other - digit) * stride
            at = base + other * count if cut else base
            copies.append(
                self.ctx["sems"].copy(
                    src.at[pl.ds(at, count), self.lines],
                    self.landed[s].at[j, :, self.lines],
                    peer,
                )
            )
        self.waiting = copies

    def receive(self, s):
        r, _ = self.ctx["stages"][s]
        digit = self.ctx["digits"][s]
        cut, count = self.plan[s]
        src, base = self.now
        for c in self.waiting:
            c.wait_recv()
        at = base + digit * count if cut else base
        own = src[pl.ds(at, count), self.lines]
        landed = self.landed[s]
        if cut:
            total = own
            for j in range(1, r):
                total = total + landed[j, :, self.lines]
        else:
            landed[0, :, self.lines] = own
            total = landed[pl.ds(digit, 1), :, self.lines][0]
            for i in range(1, r):
                total = total + landed[pl.ds(lax.rem(digit + r - i, r), 1), :, self.lines][0]
        self.held[s][:, self.lines] = total
        self.now = (self.held[s], 0)


def spread(ctx, plan, whole):
    levels = [s for s, (cut, _) in enumerate(plan) if cut]
    size = plan[-1][1]

    def where(digits):
        at, weight = 0, size
        for s in reversed(levels):
            at = at + digits[s] * weight
            weight *= ctx["stages"][s][0]
        return at

    own = {s: ctx["digits"][s] for s in levels}
    arriving = {s: [] for s in levels}

    def forward(digits, below):
        for s in reversed(below):
            r, stride = ctx["stages"][s]
            digit = ctx["digits"][s]
            for j in range(1, r):
                peer = ctx["me"] + (lax.rem(digit + j, r) - digit) * stride
                block = whole.at[pl.ds(where(digits), size)]
                c = ctx["sems"].copy(block, block, peer)
                source = dict(digits)
                source[s] = lax.rem(digit + r - j, r)
                arriving[s].append((c, source))

    def run():
        for i in reversed(range(len(levels))):
            for c, digits in arriving[levels[i]]:
                c.wait_recv()
                forward(digits, levels[:i])

    forward(own, levels)
    return where(own), run


def exchange(basis, devices, parts, iters, halves, part_ref, gram_ref, multi_ref, out_ref, *scratch):
    scratch = list(scratch)
    resp, height = part_ref.shape[0], basis.height
    cands = multi_ref.shape[1]
    stages = radices(devices)
    me = lax.axis_index("samp")
    digits = [lax.rem(me // stride, r) for r, stride in stages]
    send, recv, total, gram, maps, hot = scratch[:6]
    buffers = scratch[6:]
    k = len(stages)
    held, landed, gheld, glanded = (buffers[i * k : (i + 1) * k] for i in range(4))

    barrier = pltpu.get_barrier_semaphore()
    peers = 0
    for (r, stride), digit in zip(stages, digits):
        for j in range(1, r):
            peer = me + (lax.rem(digit + j, r) - digit) * stride
            pl.semaphore_signal(barrier, inc=1, device_id=(peer,), device_id_type=MESH)
            peers += 1
    pl.semaphore_wait(barrier, peers)

    ctx = {
        "me": me,
        "digits": digits,
        "stages": stages,
        "sems": Semaphores(send, recv),
        "counts": {id(part_ref): resp, id(gram_ref): gram_ref.shape[0]},
    }
    high = height // parts
    grams = Stream(ctx, gram_ref, slice(0, gram_ref.shape[1]), 0, gheld, glanded)
    streams = [grams] + [
        Stream(ctx, part_ref, slice(p * high, (p + 1) * high), 0, held, landed) for p in range(parts)
    ]
    for s in streams:
        s.send(0)

    line, lane = place(multi_ref[...], basis)
    maps[...] = jnp.zeros_like(maps)
    maps[0:1, 0:cands] = line
    maps[1:2, 0:cands] = lane
    for c in range(0, maps.shape[1], LANES):
        at = maps[0:1, c : c + LANES]
        row = lax.broadcasted_iota(jnp.int32, (height, LANES), 0).astype(jnp.float32)
        one = jnp.where(row == at, 1.0, 0.0).astype(jnp.bfloat16)
        for i in range(3):
            hot[i * height : (i + 1) * height, c : c + LANES] = one

    for stage in range(k):
        for s in streams:
            s.receive(stage)
            if stage + 1 < k:
                s.send(stage + 1)

    def arrange(row, store):
        first, rest = split(row)
        _, third = split(row - first.astype(jnp.float32))
        stacked = jnp.concatenate([first, rest, third], axis=0)
        wide = 4 * LANES
        for c in range(0, maps.shape[1], wide):
            size = min(wide, maps.shape[1] - c)
            found = lax.dot_general(
                stacked, hot[:, c : c + size], TN, preferred_element_type=jnp.float32
            )
            for i in range(0, size, LANES):
                at = maps[1:2, c + i : c + i + LANES]
                lo = lax.broadcasted_iota(jnp.int32, (LANES, LANES), 0).astype(jnp.float32)
                kept = jnp.where(lo == at, found[:, i : i + LANES], 0.0)
                store((c + i) // LANES, jnp.sum(kept, axis=0, keepdims=True))

    gplan, plan = grams.plan, streams[1].plan
    last, _ = grams.now
    gdigits = [s for s, (cut, _) in enumerate(gplan) if cut]
    at, weight = 0, gplan[-1][1]
    for s in reversed(gdigits):
        at = at + digits[s] * weight
        weight *= stages[s][0]
    gram[pl.ds(at, gplan[-1][1])] = last[...]
    _, run_gram = spread(ctx, gplan, gram)

    count = plan[-1][1]
    at, weight = 0, count
    for s in reversed([s for s, (cut, _) in enumerate(plan) if cut]):
        at = at + digits[s] * weight
        weight *= stages[s][0]
    reduced = held[-1]
    for i in range(count):
        row = reduced[i]
        total[pl.ds(at + i, 1)] = row[None]

        def store(b, value, i=i):
            total[pl.ds(at + i, 1), b : b + 1, :] = value[None]

        arrange(row, store)
    _, run = spread(ctx, plan, total)
    run_gram()
    for g in range(iters):
        row = jnp.concatenate([gram[g * halves + h] for h in range(halves)], axis=0)

        def store(b, value, g=g):
            out_ref[resp + g, b : b + 1, :] = value

        out_ref[resp + g] = row
        arrange(row, store)
    run()
    for g in range(iters, out_ref.shape[0] - resp):
        out_ref[resp + g] = jnp.zeros((height, LANES), jnp.float32)
    out_ref[0:resp] = total[...]
    for c in ctx["sems"].sent:
        c.wait_send()


def finish(cands, samples, iters, height, chosen_ref, total_ref, res_ref, active_ref, out_ref, corr_ref, coef_ref, flat):
    resp = res_ref.shape[0]
    for b in range(flat.shape[1] // LANES):
        for q in range(0, flat.shape[0], 8):
            flat[q : q + 8, b * LANES : (b + 1) * LANES] = total_ref[
                pl.ds(q * height + b, 8, stride=height), :
            ]
    sq = jnp.concatenate(
        [total_ref[pl.ds(q * height + height - 1, 8, stride=height), :] for q in range(0, resp, 8)],
        axis=0,
    )[:, 0:1]
    total = flat[:, 0:cands]
    column = lax.broadcasted_iota(jnp.int32, total.shape, 1)
    picked = [
        jnp.sum(jnp.where(column == chosen_ref[i], total, 0.0), axis=1, keepdims=True)
        for i in range(iters)
    ]
    target = [p[0:resp] for p in picked]
    gram = [[picked[j][resp + i : resp + i + 1] for j in range(iters)] for i in range(iters)]
    tri = [[None] * iters for _ in range(iters)]
    for i in range(iters):
        for j in range(i + 1):
            s = gram[i][j]
            for m in range(j):
                s = s - tri[i][m] * tri[j][m]
            tri[i][j] = jnp.sqrt(s) if i == j else s / tri[j][j]
    corr = total[0:resp]
    rows = [total[resp + i : resp + i + 1] for i in range(iters)]
    coef = [jnp.zeros((resp, 1), jnp.float32) for _ in range(iters)]
    for k in range(iters):
        norm = math.sqrt(samples) * jnp.sqrt(sq / samples + 1e-06)
        corr_ref[k] = corr * (1.0 / norm)
        largest = jnp.max(jnp.abs(corr), axis=1, keepdims=True)
        gamma = jnp.abs(target[k]) / (largest + 1e-06)
        w = []
        for i in range(k + 1):
            s = target[i]
            for m in range(i):
                s = s - tri[i][m] * w[m]
            w.append(s / tri[i][i])
        for i in reversed(range(k + 1)):
            s = w[i]
            for m in range(i + 1, k + 1):
                s = s - tri[m][i] * w[m]
            w[i] = s / tri[i][i]
        step = [gamma * wi for wi in w]
        for i in range(k + 1):
            coef[i] = coef[i] + step[i]
        if k < iters - 1:
            gain = sum(wi * t for wi, t in zip(w, target))
            sq = jnp.maximum(sq - gamma * (2.0 - gamma) * gain, 0.0)
            target = [
                target[j] - sum(step[i] * gram[i][j] for i in range(k + 1)) for j in range(iters)
            ]
            for i in range(k + 1):
                corr = corr - step[i] * rows[i]
    res = res_ref[...]
    active = active_ref[...].astype(jnp.float32)
    for i in range(iters):
        res = res - coef[i] * active[i : i + 1]
    out_ref[...] = res
    shape = (resp, resp)
    eye = lax.broadcasted_iota(jnp.int32, shape, 0) == lax.broadcasted_iota(jnp.int32, shape, 1)
    lines = [jnp.sum(jnp.where(eye, c, 0.0), axis=0, keepdims=True) for c in coef]
    line = lax.broadcasted_iota(jnp.int32, coef_ref.shape, 0)
    coef_ref[...] = sum(jnp.where(line == i, lines[i], 0.0) for i in range(iters))


def on_device(inputs, response, multi_index, chosen):
    nvars, width = inputs.shape
    devices = lax.axis_size("samp")
    samples = width * devices
    cands = multi_index.shape[0]
    iters = chosen.shape[0]
    resp = response.shape[0]
    basis = Basis(nvars)
    height, stride = basis.height, basis.stride
    few = up(iters, 16)
    kept = up(iters, 4)
    extra = up(kept, 8)
    used = resp + extra
    multi = multi_index.T
    vmem = pl.BlockSpec(memory_space=pltpu.VMEM)
    smem = pl.BlockSpec(memory_space=pltpu.SMEM)
    deep = math.gcd(width, 512)
    local, active = pl.pallas_call(
        functools.partial(correlate, basis, iters, deep),
        in_specs=[smem, vmem, vmem, vmem],
        out_specs=[vmem, vmem],
        out_shape=[
            jax.ShapeDtypeStruct((used * height, LANES), jnp.float32),
            jax.ShapeDtypeStruct((few, width), jnp.bfloat16),
        ],
        scratch_shapes=[
            pltpu.VMEM((3 * stride, width), jnp.float32),
            pltpu.VMEM((2 * nvars * stride, width), jnp.float32),
            pltpu.VMEM((up(2 * resp + few, LANES), width), jnp.bfloat16),
            pltpu.VMEM((basis.lines * LANES, LANES), jnp.float32),
        ],
        compiler_params=pltpu.CompilerParams(vmem_limit_bytes=VMEM_LIMIT),
        name="correlate",
    )(chosen, inputs, response, multi)

    halves = 2
    part = local[: resp * height].reshape(resp, height, LANES)
    gram = local[resp * height : (resp + kept) * height]
    gram = gram.reshape(kept * halves, height // halves, LANES)
    stages = radices(devices)
    parts = 2
    plan, gplan = halving(resp, stages), halving(gram.shape[0], stages)
    copies = (parts + 1) * sum(r - 1 for r, _ in stages)
    copies += resp // plan[-1][1] + gram.shape[0] // gplan[-1][1] - 2
    grid = up(cands, LANES)
    held = [pltpu.VMEM((c, height, LANES), jnp.float32) for _, c in plan]
    landed = [pltpu.VMEM((r, c, height, LANES), jnp.float32) for (r, _), (_, c) in zip(stages, plan)]
    unit = gram.shape[1:]
    gheld = [pltpu.VMEM((c, *unit), jnp.float32) for _, c in gplan]
    glanded = [pltpu.VMEM((r, c, *unit), jnp.float32) for (r, _), (_, c) in zip(stages, gplan)]
    total = pl.pallas_call(
        functools.partial(exchange, basis, devices, parts, iters, halves),
        in_specs=[vmem, vmem, vmem],
        out_specs=vmem,
        out_shape=jax.ShapeDtypeStruct((used, height, LANES), jnp.float32),
        scratch_shapes=[
            pltpu.SemaphoreType.DMA((copies,)),
            pltpu.SemaphoreType.DMA((copies,)),
            pltpu.VMEM((resp, height, LANES), jnp.float32),
            pltpu.VMEM(gram.shape, jnp.float32),
            pltpu.VMEM((8, grid), jnp.float32),
            pltpu.VMEM((3 * height, grid), jnp.bfloat16),
            *held,
            *landed,
            *gheld,
            *glanded,
        ],
        compiler_params=pltpu.CompilerParams(
            vmem_limit_bytes=VMEM_LIMIT, collective_id=0, has_side_effects=True
        ),
        name="exchange",
    )(part, gram, multi)
    residual, corr, coef = pl.pallas_call(
        functools.partial(finish, cands, samples, iters, height),
        in_specs=[smem, vmem, vmem, vmem],
        out_specs=[vmem, vmem, vmem],
        out_shape=[
            jax.ShapeDtypeStruct((resp, width), jnp.float32),
            jax.ShapeDtypeStruct((iters, resp, cands), jnp.float32),
            jax.ShapeDtypeStruct((extra, resp), jnp.float32),
        ],
        scratch_shapes=[pltpu.VMEM((used, grid), jnp.float32)],
        compiler_params=pltpu.CompilerParams(vmem_limit_bytes=VMEM_LIMIT),
        name="finish",
    )(chosen, total.reshape(used * height, LANES), response, active)
    return residual, corr, coef[:iters]


def solution(mesh):
    placed = (P(None, "samp"), P(None, "samp"), P(), P())
    return jax.shard_map(
        on_device,
        mesh=mesh,
        in_specs=placed,
        out_specs=(P(None, "samp"), P(), P()),
        check_vma=False,
    )
```

time: 194 us -> 54.4 us (0.28)
  waiting for transfers between devices: 133 us -> 0 us
  between operations: 14.1 us -> 0.64 us
  Pallas kernels: 36.4 us -> 48.5 us
  local copies, waits for them, and re-layouts: 10.1 us -> 4.9 us
    psum x1 -> x0, waiting for transfers between devices: 133 us -> none  [on_device(): total = lax.psum(local, 'samp')]
    pallas_call x2 -> x3, Pallas kernels: 36.4 us -> 48.5 us  [the longest x1 32.2 us: on_device(): pl.pallas_call(functools.partial(exchange, basis, devices, parts, iters,...]
    unnamed x11 -> x0, local copies, waits for them, and re-layouts: 5.12 us -> none
    slice x0 -> x2, local copies, waits for them, and re-layouts: none -> 3.64 us  [the longest x1 2.1 us: on_device(): part = local[:resp * height].reshape(resp, height, LANES)]
    gather x1 -> x0, local copies, waits for them, and re-layouts: 2.35 us -> none  [on_device(): picked = jnp.pad(multi_index[chosen], ((0, few - iters), (0, 0)))]
    pad x3 -> x0, local copies, waits for them, and re-layouts: 2.06 us -> none  [the longest x1 2.03 us: on_device(): jnp.pad(multi_index, ((0, padded - cands), (0, 0)))]
  transfers between devices with their start and end apart: 1 -> 0, of which waited for: 1 -> 0; matrix products, arithmetic and copies ran while one was open for 0% -> 0% of each run, Pallas kernels for 0% -> 0%
where the time goes in v1:
time: 54.4 us; the launch traced here: 54.1 us
  Pallas kernels  48.5 us (89%)
  local copies, waits for them, and re-layouts  4.9 us (9%)
  between operations  0.64 us (1%)
    pallas_call x1, Pallas kernels, on_device(): pl.pallas_call(functools.partial(exchange, basis, devices, parts, iters,...  32.2 us
    pallas_call x1, Pallas kernels, on_device(): pl.pallas_call(functools.partial(correlate, basis, iters, deep), in_specs...  12.7 us
    pallas_call x1, Pallas kernels, on_device(): pl.pallas_call(functools.partial(finish, cands, samples, iters, height),...  3.69 us
    slice x1, local copies, waits for them, and re-layouts, on_device(): part = local[:resp * height].reshape(resp, height, LANES)  2.1 us
    slice x1, local copies, waits for them, and re-layouts, on_device(): gram = local[resp * height:(resp + kept) * height]  1.54 us
    slice x1, local copies, waits for them, and re-layouts, on_device(): return (residual, corr, coef[:iters])  1.26 us

profile of v1, /device:TPU:0, one launch (start us, length us, event | category | flops | bytes accessed | tf_op | source)
XLA Modules:
  0.0 54.1 jit_solution(9244954897998630530)
XLA Ops:
  0.6 12.7 %correlate.1 = (f32[1920,128]{1,0:T(8,128)}, bf16[16,2048]{1,0:T(8,128)(2,1)}) custom-call(s32[3]{0:T(128)} %chosen_ref.3, f32[30,2048]{1,0:T(8,128)} %x_ref.1, f32[32,2048]{1,0:T(8,128)} %res_ref.3, s32[30,5456]{1,0:T(8,128)} %bitcast.6), custom_call_target="tpu_custom_call" | custom-call | tf_op jit(solution)/shard_map/correlate/pallas_call | solution.py:520
  13.3 1.5 %slice.10 = f32[192,128]{1,0:T(8,128)} slice(f32[1920,128]{1,0:T(8,128)} %get-tuple-element.8), slice={[1536:1728], [0:128]} | slice | bytes 196608 | tf_op jit(solution)/shard_map/slice | solution.py:540
  14.9 2.1 %slice.9 = f32[1536,128]{1,0:T(8,128)} slice(f32[1920,128]{1,0:T(8,128)} %get-tuple-element.8), slice={[0:1536], [0:128]} | slice | bytes 1572864 | tf_op jit(solution)/shard_map/slice | solution.py:539
  17.0 32.2 %exchange.1 = f32[40,48,128]{2,1,0:T(8,128)} custom-call(f32[32,48,128]{2,1,0:T(8,128)} %bitcast.5, f32[8,24,128]{2,1,0:T(8,128)} %bitcast.8, s32[30,5456]{1,0:T(8,128)} %bitcast.7), custom_call_target="tpu_custom_call" | custom-call | tf_op jit(solution)/shard_map/exchange/pallas_call | solution.py:553
  49.1 3.7 %finish.1 = (f32[32,2048]{1,0:T(8,128)}, f32[3,32,5456]{2,1,0:T(8,128)}, f32[8,32]{1,0:T(8,128)}) custom-call(s32[3]{0:T(128)} %chosen_ref.3, f32[1920,128]{1,0:T(8,128)} %bitcast.4, f32[32,2048]{1,0:T(8,128)} %res_ref.3, bf16[16,2048]{1,0:T(8,128)(2,1)} %get-tuple-element.9.active_ref), custom_call_target="tpu_custom_call" | custom-call | tf_op jit(solution)/shard_map/finish/pallas_call | solution.py:575
  52.8 1.3 %slice.11 = f32[3,32]{1,0:T(4,128)} slice(f32[8,32]{1,0:T(8,128)} %get-tuple-element.12), slice={[0:3], [0:32]} | slice | bytes 768 | tf_op jit(solution)/shard_map/slice | solution.py:588

commit v2 on v1

--- a/solution.py
+++ b/solution.py
@@ -89,7 +89,7 @@
     return line, index - line * float(LANES)
 
 
-def correlate(basis, iters, deep, chosen_ref, x_ref, res_ref, multi_ref, out_ref, active_ref, twice, turned, rows, acc):
+def prepare(basis, iters, chosen_ref, x_ref, res_ref, multi_ref, active_ref, twice, turned, rows):
     nvars, width = x_ref.shape
     resp = res_ref.shape[0]
     stride = basis.stride
@@ -98,20 +98,16 @@
     second = (3.0 * x * x - 1.0) * 0.5
     third = (5.0 * x * x * x - 3.0 * x) * 0.5
     values = [x * math.sqrt(3.0), second * math.sqrt(5.0), third * math.sqrt(7.0)]
-    tall = twice.shape[0] // 3
     for e, value in enumerate(values):
-        twice[e * tall : (e + 1) * tall, :] = jnp.ones((tall, width), jnp.float32)
-        twice[e * tall : e * tall + nvars, :] = value
-    for d in range(nvars):
-        if d:
-            turned[d * stride : d * stride + nvars - d, :] = values[0][d:]
-            turned[d * stride + nvars - d : d * stride + nvars, :] = values[0][:d]
-            turned[(nvars + d) * stride : (nvars + d) * stride + nvars - d, :] = values[1][d:]
-            turned[(nvars + d) * stride + nvars - d : (nvars + d) * stride + nvars, :] = values[1][:d]
+        twice[e * stride + nvars : (e + 1) * stride, :] = jnp.ones((stride - nvars, width), jnp.float32)
+        twice[e * stride : e * stride + nvars, :] = value
     zero = jnp.zeros((stride - nvars, width), jnp.float32)
-    for d in range(1, nvars):
-        turned[d * stride + nvars : (d + 1) * stride, :] = zero
-        turned[(nvars + d) * stride + nvars : (nvars + d + 1) * stride, :] = zero
+    for e in range(2):
+        for d in range(1, nvars):
+            at = (e * nvars + d) * stride
+            turned[at : at + nvars - d, :] = values[e][d:]
+            turned[at + nvars - d : at + nvars, :] = values[e][:d]
+            turned[at + nvars : at + stride, :] = zero
 
     high, low = split(res_ref[...])
     rows[0:resp, :] = high
@@ -144,14 +140,19 @@
     rest = rows.shape[0] - 2 * resp - few
     rows[2 * resp + few :, :] = jnp.zeros((rest, width), jnp.bfloat16)
 
+
+def correlate(basis, blocks, deep, twice, turned, rows, acc):
+    stride, nvars = basis.stride, basis.nvars
+    width = rows.shape[1]
     per = 512 // stride
-    groups = [basis.blocks[i : i + per] for i in range(0, len(basis.blocks), per)]
+    groups = [blocks[i : i + per] for i in range(0, len(blocks), per)]
 
     def step(k, first):
         for g, group in enumerate(groups):
             total = None
             for half in range(0, deep, 256):
-                cols = pl.ds(pl.multiple_of(k * deep + half, 256), 256)
+                at = k * deep + half
+                cols = pl.ds(at if first else pl.multiple_of(at, 256), 256)
                 f1 = twice[0:stride, cols]
                 parts = []
                 held = None
@@ -166,7 +167,7 @@
                     elif kind == "square":
                         part = f1 * turned[(nvars + d) * stride : (nvars + d + 1) * stride, cols]
                     else:
-                        part = twice[d * tall : d * tall + stride, cols]
+                        part = twice[d * stride : (d + 1) * stride, cols]
                     parts.append(part.astype(jnp.bfloat16))
                 psi = jnp.concatenate(parts, axis=0)
                 term = lax.dot_general(psi, rows[:, cols], NT, preferred_element_type=jnp.float32)
@@ -176,23 +177,11 @@
 
     step(0, True)
 
-    @pl.loop(1, width // deep)
-    def _(k):
-        step(k, False)
-
-    height = basis.height
-    for b in range(basis.lines):
-        t = acc[b * LANES : (b + 1) * LANES, :].T
-        corr = t[0:resp] + t[resp : 2 * resp]
-        for q in range(0, resp, 8):
-            out_ref[pl.ds(q * height + b, 8, stride=height), :] = corr[q : q + 8]
-        out_ref[pl.ds(resp * height + b, 8, stride=height), :] = t[2 * resp : 2 * resp + 8]
-    res = res_ref[...]
-    sq = jnp.broadcast_to(jnp.sum(res * res, axis=1, keepdims=True), (resp, LANES))
-    for b in range(basis.lines, height):
-        for q in range(0, resp, 8):
-            out_ref[pl.ds(q * height + b, 8, stride=height), :] = sq[q : q + 8]
-        out_ref[pl.ds(resp * height + b, 8, stride=height), :] = jnp.zeros((8, LANES), jnp.float32)
+    if width > deep:
+
+        @pl.loop(1, width // deep)
+        def _(k):
+            step(k, False)
 
 
 def radices(n):
@@ -236,28 +225,26 @@
 
 
 class Stream:
-    def __init__(self, ctx, part, lines, offset, held, landed):
-        self.ctx, self.lines = ctx, lines
-        self.now = (part, offset)
+    def __init__(self, ctx, part, count, unit, held, landed):
+        self.ctx, self.unit = ctx, unit
+        self.now = part
         self.held, self.landed = held, landed
-        self.plan = halving(ctx["counts"][id(part)], ctx["stages"])
+        self.plan = halving(count, ctx["stages"])
         self.waiting = None
 
     def send(self, s):
         r, stride = self.ctx["stages"][s]
         digit = self.ctx["digits"][s]
         cut, count = self.plan[s]
-        src, base = self.now
+        size = count * self.unit
         copies = []
         for j in range(1, r):
             other = lax.rem(digit + j, r)
             peer = self.ctx["me"] + (other - digit) * stride
-            at = base + other * count if cut else base
+            at = pl.multiple_of(other * size, 8) if cut else 0
             copies.append(
                 self.ctx["sems"].copy(
-                    src.at[pl.ds(at, count), self.lines],
-                    self.landed[s].at[j, :, self.lines],
-                    peer,
+                    self.now.at[pl.ds(at, size)], self.landed[s].at[pl.ds(j * size, size)], peer
                 )
             )
         self.waiting = copies
@@ -266,46 +253,49 @@
         r, _ = self.ctx["stages"][s]
         digit = self.ctx["digits"][s]
         cut, count = self.plan[s]
-        src, base = self.now
+        size = count * self.unit
         for c in self.waiting:
             c.wait_recv()
-        at = base + digit * count if cut else base
-        own = src[pl.ds(at, count), self.lines]
+        at = pl.multiple_of(digit * size, 8) if cut else 0
+        own = self.now[pl.ds(at, size), :]
         landed = self.landed[s]
         if cut:
             total = own
             for j in range(1, r):
-                total = total + landed[j, :, self.lines]
+                total = total + landed[j * size : (j + 1) * size, :]
         else:
-            landed[0, :, self.lines] = own
-            total = landed[pl.ds(digit, 1), :, self.lines][0]
-            for i in range(1, r):
-                total = total + landed[pl.ds(lax.rem(digit + r - i, r), 1), :, self.lines][0]
-        self.held[s][:, self.lines] = total
-        self.now = (self.held[s], 0)
-
-
-def spread(ctx, plan, whole):
-    levels = [s for s, (cut, _) in enumerate(plan) if cut]
-    size = plan[-1][1]
-
-    def where(digits):
-        at, weight = 0, size
-        for s in reversed(levels):
+            landed[0:size, :] = own
+            total = None
+            for i in range(r):
+                at = pl.multiple_of(lax.rem(digit + r - i, r) * size, 8)
+                term = landed[pl.ds(at, size), :]
+                total = term if total is None else total + term
+        self.held[s][...] = total
+        self.now = self.held[s]
+
+
+def digit_place(ctx, plan, digits):
+    at, weight = 0, plan[-1][1]
+    for s in reversed(range(len(plan))):
+        if plan[s][0]:
             at = at + digits[s] * weight
             weight *= ctx["stages"][s][0]
-        return at
-
-    own = {s: ctx["digits"][s] for s in levels}
+    return at
+
+
+def spread(ctx, plan, unit, whole):
+    levels = [s for s, (cut, _) in enumerate(plan) if cut]
+    size = plan[-1][1] * unit
     arriving = {s: [] for s in levels}
 
     def forward(digits, below):
+        at = pl.multiple_of(digit_place(ctx, plan, digits) * unit, 8)
+        block = whole.at[pl.ds(at, size)]
         for s in reversed(below):
             r, stride = ctx["stages"][s]
             digit = ctx["digits"][s]
             for j in range(1, r):
                 peer = ctx["me"] + (lax.rem(digit + j, r) - digit) * stride
-                block = whole.at[pl.ds(where(digits), size)]
                 c = ctx["sems"].copy(block, block, peer)
                 source = dict(digits)
                 source[s] = lax.rem(digit + r - j, r)
@@ -317,21 +307,26 @@
                 c.wait_recv()
                 forward(digits, levels[:i])
 
-    forward(own, levels)
-    return where(own), run
-
-
-def exchange(basis, devices, parts, iters, halves, part_ref, gram_ref, multi_ref, out_ref, *scratch):
+    forward(dict(enumerate(ctx["digits"])), levels)
+    return run
+
+
+def learn(basis, devices, parts, iters, deep, halves, chosen_ref, x_ref, res_ref, multi_ref, out_ref, active_ref, *scratch):
     scratch = list(scratch)
-    resp, height = part_ref.shape[0], basis.height
+    resp, height = res_ref.shape[0], basis.height
+    high = height // parts
     cands = multi_ref.shape[1]
     stages = radices(devices)
     me = lax.axis_index("samp")
     digits = [lax.rem(me // stride, r) for r, stride in stages]
-    send, recv, total, gram, maps, hot = scratch[:6]
-    buffers = scratch[6:]
+    send, recv, twice, turned, rows, acc, total, gram, whole_gram, maps, hot = scratch[:11]
+    buffers = scratch[11:]
     k = len(stages)
-    held, landed, gheld, glanded = (buffers[i * k : (i + 1) * k] for i in range(4))
+    take = lambda n: [buffers.pop(0) for _ in range(n)]
+    part = take(parts)
+    held = [take(k) for _ in range(parts)]
+    landed = [take(k) for _ in range(parts)]
+    gheld, glanded = take(k), take(k)
 
     barrier = pltpu.get_barrier_semaphore()
     peers = 0
@@ -340,39 +335,65 @@
             peer = me + (lax.rem(digit + j, r) - digit) * stride
             pl.semaphore_signal(barrier, inc=1, device_id=(peer,), device_id_type=MESH)
             peers += 1
-    pl.semaphore_wait(barrier, peers)
-
-    ctx = {
-        "me": me,
-        "digits": digits,
-        "stages": stages,
-        "sems": Semaphores(send, recv),
-        "counts": {id(part_ref): resp, id(gram_ref): gram_ref.shape[0]},
-    }
-    high = height // parts
-    grams = Stream(ctx, gram_ref, slice(0, gram_ref.shape[1]), 0, gheld, glanded)
-    streams = [grams] + [
-        Stream(ctx, part_ref, slice(p * high, (p + 1) * high), 0, held, landed) for p in range(parts)
-    ]
-    for s in streams:
-        s.send(0)
+
+    ctx = {"me": me, "digits": digits, "stages": stages, "sems": Semaphores(send, recv)}
+    kept = up(iters, 4)
+    unit = height // halves
+    grams = Stream(ctx, gram, kept * halves, unit, gheld, glanded)
+    streams = [Stream(ctx, part[p], resp, high, held[p], landed[p]) for p in range(parts)]
+
+    prepare(basis, iters, chosen_ref, x_ref, res_ref, multi_ref, active_ref, twice, turned, rows)
+    per = high * LANES // basis.stride
+    for p in range(parts):
+        blocks = basis.blocks[p * per : (p + 1) * per]
+        correlate(basis, blocks, deep, twice, turned, rows, acc)
+        count = len(blocks) * basis.stride // LANES
+        for b in range(count):
+            t = acc[b * LANES : (b + 1) * LANES, :].T
+            corr = t[0:resp] + t[resp : 2 * resp]
+            for q in range(0, resp, 8):
+                part[p][pl.ds(q * high + b, 8, stride=high), :] = corr[q : q + 8]
+            gram[pl.ds(p * high + b, 8, stride=height), :] = t[2 * resp : 2 * resp + 8]
+        if count < high:
+            res = res_ref[...]
+            sq = jnp.broadcast_to(jnp.sum(res * res, axis=1, keepdims=True), (resp, LANES))
+            for b in range(count, high):
+                for q in range(0, resp, 8):
+                    part[p][pl.ds(q * high + b, 8, stride=high), :] = sq[q : q + 8]
+                gram[pl.ds(p * high + b, 8, stride=height), :] = jnp.zeros((8, LANES), jnp.float32)
+        if p == 0:
+            pl.semaphore_wait(barrier, peers)
+        else:
+            streams[p - 1].receive(0)
+            if k > 1:
+                streams[p - 1].send(1)
+        streams[p].send(0)
+    grams.send(0)
 
     line, lane = place(multi_ref[...], basis)
     maps[...] = jnp.zeros_like(maps)
     maps[0:1, 0:cands] = line
     maps[1:2, 0:cands] = lane
+    for s in streams[parts - 1 :] + [grams]:
+        s.receive(0)
+        if k > 1:
+            s.send(1)
     for c in range(0, maps.shape[1], LANES):
         at = maps[0:1, c : c + LANES]
         row = lax.broadcasted_iota(jnp.int32, (height, LANES), 0).astype(jnp.float32)
         one = jnp.where(row == at, 1.0, 0.0).astype(jnp.bfloat16)
         for i in range(3):
             hot[i * height : (i + 1) * height, c : c + LANES] = one
-
-    for stage in range(k):
-        for s in streams:
+    for stage in range(1, k):
+        for s in streams + [grams]:
             s.receive(stage)
             if stage + 1 < k:
                 s.send(stage + 1)
+
+    gplan, plan = grams.plan, streams[0].plan
+    at = pl.multiple_of(digit_place(ctx, gplan, digits) * unit, 8)
+    whole_gram[pl.ds(at, gplan[-1][1] * unit), :] = grams.now[...]
+    run_gram = spread(ctx, gplan, unit, whole_gram)
 
     def arrange(row, store):
         first, rest = split(row)
@@ -390,44 +411,28 @@
                 kept = jnp.where(lo == at, found[:, i : i + LANES], 0.0)
                 store((c + i) // LANES, jnp.sum(kept, axis=0, keepdims=True))
 
-    gplan, plan = grams.plan, streams[1].plan
-    last, _ = grams.now
-    gdigits = [s for s, (cut, _) in enumerate(gplan) if cut]
-    at, weight = 0, gplan[-1][1]
-    for s in reversed(gdigits):
-        at = at + digits[s] * weight
-        weight *= stages[s][0]
-    gram[pl.ds(at, gplan[-1][1])] = last[...]
-    _, run_gram = spread(ctx, gplan, gram)
-
-    count = plan[-1][1]
-    at, weight = 0, count
-    for s in reversed([s for s, (cut, _) in enumerate(plan) if cut]):
-        at = at + digits[s] * weight
-        weight *= stages[s][0]
-    reduced = held[-1]
-    for i in range(count):
-        row = reduced[i]
-        total[pl.ds(at + i, 1)] = row[None]
-
-        def store(b, value, i=i):
-            total[pl.ds(at + i, 1), b : b + 1, :] = value[None]
-
-        arrange(row, store)
-    _, run = spread(ctx, plan, total)
+    mine = digit_place(ctx, plan, digits) * height
+    for i in range(plan[-1][1]):
+        row = jnp.concatenate([s.now[i * high : (i + 1) * high, :] for s in streams], axis=0)
+        lines = [row[height - 1 :]] * (height - maps.shape[1] // LANES)
+        found = {}
+        arrange(row, found.__setitem__)
+        row = jnp.concatenate([found[b] for b in range(len(found))] + lines, axis=0)
+        total[pl.ds(pl.multiple_of(mine + i * height, 8), height), :] = row
+    run = spread(ctx, plan, height, total)
     run_gram()
     for g in range(iters):
-        row = jnp.concatenate([gram[g * halves + h] for h in range(halves)], axis=0)
-
-        def store(b, value, g=g):
-            out_ref[resp + g, b : b + 1, :] = value
-
-        out_ref[resp + g] = row
-        arrange(row, store)
+        row = whole_gram[g * height : (g + 1) * height, :]
+        found = {}
+        arrange(row, found.__setitem__)
+        lines = [row[height - 1 :]] * (height - len(found))
+        out_ref[(resp + g) * height : (resp + g + 1) * height, :] = jnp.concatenate(
+            [found[b] for b in range(len(found))] + lines, axis=0
+        )
     run()
-    for g in range(iters, out_ref.shape[0] - resp):
-        out_ref[resp + g] = jnp.zeros((height, LANES), jnp.float32)
-    out_ref[0:resp] = total[...]
+    rest = out_ref.shape[0] - (resp + iters) * height
+    out_ref[(resp + iters) * height :, :] = jnp.zeros((rest, LANES), jnp.float32)
+    out_ref[0 : resp * height, :] = total[...]
     for c in ctx["sems"].sent:
         c.wait_send()
 
@@ -517,8 +522,20 @@
     vmem = pl.BlockSpec(memory_space=pltpu.VMEM)
     smem = pl.BlockSpec(memory_space=pltpu.SMEM)
     deep = math.gcd(width, 512)
-    local, active = pl.pallas_call(
-        functools.partial(correlate, basis, iters, deep),
+    halves, parts = 2, 3
+    high, unit = height // parts, height // halves
+    stages = radices(devices)
+    plan, gplan = halving(resp, stages), halving(kept * halves, stages)
+    copies = (parts + 1) * sum(r - 1 for r, _ in stages)
+    copies += resp // plan[-1][1] + kept * halves // gplan[-1][1] - 2
+    grid = up(cands, LANES)
+    lines = lambda n: pltpu.VMEM((n, LANES), jnp.float32)
+    held = [lines(c * high) for _, c in plan]
+    landed = [lines(r * c * high) for (r, _), (_, c) in zip(stages, plan)]
+    gheld = [lines(c * unit) for _, c in gplan]
+    glanded = [lines(r * c * unit) for (r, _), (_, c) in zip(stages, gplan)]
+    total, active = pl.pallas_call(
+        functools.partial(learn, basis, devices, parts, iters, deep, halves),
         in_specs=[smem, vmem, vmem, vmem],
         out_specs=[vmem, vmem],
         out_shape=[
@@ -526,52 +543,28 @@
             jax.ShapeDtypeStruct((few, width), jnp.bfloat16),
         ],
         scratch_shapes=[
+            pltpu.SemaphoreType.DMA((copies,)),
+            pltpu.SemaphoreType.DMA((copies,)),
             pltpu.VMEM((3 * stride, width), jnp.float32),
             pltpu.VMEM((2 * nvars * stride, width), jnp.float32),
             pltpu.VMEM((up(2 * resp + few, LANES), width), jnp.bfloat16),
-            pltpu.VMEM((basis.lines * LANES, LANES), jnp.float32),
-        ],
-        compiler_params=pltpu.CompilerParams(vmem_limit_bytes=VMEM_LIMIT),
-        name="correlate",
-    )(chosen, inputs, response, multi)
-
-    halves = 2
-    part = local[: resp * height].reshape(resp, height, LANES)
-    gram = local[resp * height : (resp + kept) * height]
-    gram = gram.reshape(kept * halves, height // halves, LANES)
-    stages = radices(devices)
-    parts = 2
-    plan, gplan = halving(resp, stages), halving(gram.shape[0], stages)
-    copies = (parts + 1) * sum(r - 1 for r, _ in stages)
-    copies += resp // plan[-1][1] + gram.shape[0] // gplan[-1][1] - 2
-    grid = up(cands, LANES)
-    held = [pltpu.VMEM((c, height, LANES), jnp.float32) for _, c in plan]
-    landed = [pltpu.VMEM((r, c, height, LANES), jnp.float32) for (r, _), (_, c) in zip(stages, plan)]
-    unit = gram.shape[1:]
-    gheld = [pltpu.VMEM((c, *unit), jnp.float32) for _, c in gplan]
-    glanded = [pltpu.VMEM((r, c, *unit), jnp.float32) for (r, _), (_, c) in zip(stages, gplan)]
-    total = pl.pallas_call(
-        functools.partial(exchange, basis, devices, parts, iters, halves),
-        in_specs=[vmem, vmem, vmem],
-        out_specs=vmem,
-        out_shape=jax.ShapeDtypeStruct((used, height, LANES), jnp.float32),
-        scratch_shapes=[
-            pltpu.SemaphoreType.DMA((copies,)),
-            pltpu.SemaphoreType.DMA((copies,)),
-            pltpu.VMEM((resp, height, LANES), jnp.float32),
-            pltpu.VMEM(gram.shape, jnp.float32),
+            lines(high * LANES),
+            lines(resp * height),
+            lines(up(kept, 8) * height),
+            lines(kept * height),
             pltpu.VMEM((8, grid), jnp.float32),
             pltpu.VMEM((3 * height, grid), jnp.bfloat16),
-            *held,
-            *landed,
+            *[lines(resp * high) for _ in range(parts)],
+            *(held * parts),
+            *(landed * parts),
             *gheld,
             *glanded,
         ],
         compiler_params=pltpu.CompilerParams(
             vmem_limit_bytes=VMEM_LIMIT, collective_id=0, has_side_effects=True
         ),
-        name="exchange",
-    )(part, gram, multi)
+        name="learn",
+    )(chosen, inputs, response, multi)
     residual, corr, coef = pl.pallas_call(
         functools.partial(finish, cands, samples, iters, height),
         in_specs=[smem, vmem, vmem, vmem],
@@ -579,13 +572,13 @@
         out_shape=[
             jax.ShapeDtypeStruct((resp, width), jnp.float32),
             jax.ShapeDtypeStruct((iters, resp, cands), jnp.float32),
-            jax.ShapeDtypeStruct((extra, resp), jnp.float32),
+            jax.ShapeDtypeStruct((iters, resp), jnp.float32),
         ],
         scratch_shapes=[pltpu.VMEM((used, grid), jnp.float32)],
         compiler_params=pltpu.CompilerParams(vmem_limit_bytes=VMEM_LIMIT),
         name="finish",
-    )(chosen, total.reshape(used * height, LANES), response, active)
-    return residual, corr, coef[:iters]
+    )(chosen, total, response, active)
+    return residual, corr, coef
 
 
 def solution(mesh):

time: 54.4 us -> 44.5 us (0.82)
  local copies, waits for them, and re-layouts: 4.9 us -> 0 us
  Pallas kernels: 48.5 us -> 43.7 us
    slice x3 -> x0, local copies, waits for them, and re-layouts: 4.9 us -> none  [the longest x1 2.1 us: on_device(): part = local[:resp * height].reshape(resp, height, LANES)]
    pallas_call x2 -> x1, Pallas kernels: 44.9 us -> 40 us  [on_device(): pl.pallas_call(functools.partial(learn, basis, devices, parts, iters, dee...]
where the time goes in v2:
time: 44.5 us; the launch traced here: 44.3 us
  Pallas kernels  43.7 us (98%)
  between operations  0.64 us (1%)
    pallas_call x1, Pallas kernels, on_device(): pl.pallas_call(functools.partial(learn, basis, devices, parts, iters, dee...  40 us
    pallas_call x1, Pallas kernels, on_device(): pl.pallas_call(functools.partial(finish, cands, samples, iters, height),...  3.69 us

profile of v2, /device:TPU:0, one launch (start us, length us, event | category | flops | bytes accessed | tf_op | source)
XLA Modules:
  0.0 44.3 jit_solution(15516219052875199545)
XLA Ops:
  0.6 40.0 %learn.1 = (f32[1920,128]{1,0:T(8,128)}, bf16[16,2048]{1,0:T(8,128)(2,1)}) custom-call(s32[3]{0:T(128)} %chosen_ref.3, f32[30,2048]{1,0:T(8,128)} %x_ref.1, f32[32,2048]{1,0:T(8,128)} %res_ref.3, s32[30,5456]{1,0:T(8,128)} %bitcast.1), custom_call_target="tpu_custom_call" | custom-call | tf_op jit(solution)/shard_map/learn/pallas_call | solution.py:537
  40.7 3.7 %finish.1 = (f32[32,2048]{1,0:T(8,128)}, f32[3,32,5456]{2,1,0:T(8,128)}, f32[3,32]{1,0:T(4,128)}) custom-call(s32[3]{0:T(128)} %chosen_ref.3, f32[1920,128]{1,0:T(8,128)} %get-tuple-element.5.total_ref, f32[32,2048]{1,0:T(8,128)} %res_ref.3, bf16[16,2048]{1,0:T(8,128)(2,1)} %get-tuple-element.6.active_ref), custom_call_target="tpu_custom_call" | custom-call | tf_op jit(solution)/shard_map/finish/pallas_call | solution.py:568

commit v3 on v2

--- a/solution.py
+++ b/solution.py
@@ -12,7 +12,7 @@
 NT = (((1,), (1,)), ((), ()))
 TN = (((0,), (0,)), ((), ()))
 MESH = pl.DeviceIdType.MESH
-VMEM_LIMIT = 56 * 2**20
+VMEM_LIMIT = 57 * 2**20
 
 
 def up(n, m):
@@ -45,7 +45,7 @@
         while len(self.blocks) * self.stride % LANES:
             self.blocks.append(("single", 0, 0))
         self.lines = len(self.blocks) * self.stride // LANES
-        self.height = up(self.lines + 1, 24)
+        self.height = up(self.lines + 1, 48)
 
 
 def place(multi, basis):
@@ -89,11 +89,12 @@
     return line, index - line * float(LANES)
 
 
-def prepare(basis, iters, chosen_ref, x_ref, res_ref, multi_ref, active_ref, twice, turned, rows):
+def prepare(basis, iters, loads, chosen_ref, x_ref, res_ref, multi_ref, active_ref, twice, turned, rows):
     nvars, width = x_ref.shape
     resp = res_ref.shape[0]
     stride = basis.stride
     few = active_ref.shape[0]
+    loads[0].wait()
     x = x_ref[...]
     second = (3.0 * x * x - 1.0) * 0.5
     third = (5.0 * x * x * x - 3.0 * x) * 0.5
@@ -109,6 +110,8 @@
             turned[at + nvars - d : at + nvars, :] = values[e][:d]
             turned[at + nvars : at + stride, :] = zero
 
+    loads[1].wait()
+    loads[2].wait()
     high, low = split(res_ref[...])
     rows[0:resp, :] = high
     rows[resp : 2 * resp, :] = low
@@ -238,7 +241,7 @@
         cut, count = self.plan[s]
         size = count * self.unit
         copies = []
-        for j in range(1, r):
+        for j in range(r - 1, 0, -1):
             other = lax.rem(digit + j, r)
             peer = self.ctx["me"] + (other - digit) * stride
             at = pl.multiple_of(other * size, 8) if cut else 0
@@ -283,9 +286,9 @@
     return at
 
 
-def spread(ctx, plan, unit, whole):
+def spread(ctx, plan, unit, tall, whole):
     levels = [s for s, (cut, _) in enumerate(plan) if cut]
-    size = plan[-1][1] * unit
+    size = (plan[-1][1] - 1) * unit + tall
     arriving = {s: [] for s in levels}
 
     def forward(digits, below):
@@ -294,39 +297,48 @@
         for s in reversed(below):
             r, stride = ctx["stages"][s]
             digit = ctx["digits"][s]
-            for j in range(1, r):
+            for j in range(r - 1, 0, -1):
                 peer = ctx["me"] + (lax.rem(digit + j, r) - digit) * stride
                 c = ctx["sems"].copy(block, block, peer)
                 source = dict(digits)
                 source[s] = lax.rem(digit + r - j, r)
                 arriving[s].append((c, source))
 
+    forward(dict(enumerate(ctx["digits"])), levels)
+
     def run():
         for i in reversed(range(len(levels))):
             for c, digits in arriving[levels[i]]:
                 c.wait_recv()
                 forward(digits, levels[:i])
-
-    forward(dict(enumerate(ctx["digits"])), levels)
-    return run
-
-
-def learn(basis, devices, parts, iters, deep, halves, chosen_ref, x_ref, res_ref, multi_ref, out_ref, active_ref, *scratch):
+                yield levels[i]
+
+    return run()
+
+
+def learn(basis, devices, parts, iters, deep, halves, tile, chosen_ref, x_in, res_in, multi_in, out_ref, active_ref, *scratch):
     scratch = list(scratch)
-    resp, height = res_ref.shape[0], basis.height
+    resp, height = res_in.shape[0], basis.height
     high = height // parts
-    cands = multi_ref.shape[1]
+    cands = multi_in.shape[1]
     stages = radices(devices)
     me = lax.axis_index("samp")
     digits = [lax.rem(me // stride, r) for r, stride in stages]
-    send, recv, twice, turned, rows, acc, total, gram, whole_gram, maps, hot = scratch[:11]
-    buffers = scratch[11:]
+    send, recv, loaded, x_ref, res_ref, multi_ref, twice, turned, rows, acc, total, maps, hot = scratch[:13]
+    buffers = scratch[13:]
+    loads = []
+    for i, (a, b) in enumerate([(x_in, x_ref), (multi_in, multi_ref), (res_in, res_ref)]):
+        loads.append(pltpu.make_async_copy(a, b, loaded.at[i]))
+        loads[-1].start()
     k = len(stages)
     take = lambda n: [buffers.pop(0) for _ in range(n)]
     part = take(parts)
     held = [take(k) for _ in range(parts)]
     landed = [take(k) for _ in range(parts)]
-    gheld, glanded = take(k), take(k)
+    pieces = parts // 2
+    gram, whole_gram = take(pieces), take(pieces)
+    gheld = [take(k) for _ in range(pieces)]
+    glanded = [take(k) for _ in range(pieces)]
 
     barrier = pltpu.get_barrier_semaphore()
     peers = 0
@@ -338,12 +350,16 @@
 
     ctx = {"me": me, "digits": digits, "stages": stages, "sems": Semaphores(send, recv)}
     kept = up(iters, 4)
-    unit = height // halves
-    grams = Stream(ctx, gram, kept * halves, unit, gheld, glanded)
+    unit = 2 * high // halves
+    grams = [
+        Stream(ctx, gram[g], kept * halves, unit, gheld[g], glanded[g]) for g in range(pieces)
+    ]
     streams = [Stream(ctx, part[p], resp, high, held[p], landed[p]) for p in range(parts)]
 
-    prepare(basis, iters, chosen_ref, x_ref, res_ref, multi_ref, active_ref, twice, turned, rows)
+    prepare(basis, iters, loads, chosen_ref, x_ref, res_ref, multi_ref, active_ref, twice, turned, rows)
     per = high * LANES // basis.stride
+    hold = 1
+    flying = []
     for p in range(parts):
         blocks = basis.blocks[p * per : (p + 1) * per]
         correlate(basis, blocks, deep, twice, turned, rows, acc)
@@ -353,28 +369,37 @@
             corr = t[0:resp] + t[resp : 2 * resp]
             for q in range(0, resp, 8):
                 part[p][pl.ds(q * high + b, 8, stride=high), :] = corr[q : q + 8]
-            gram[pl.ds(p * high + b, 8, stride=height), :] = t[2 * resp : 2 * resp + 8]
+            gram[p // 2][pl.ds(p % 2 * high + b, 8, stride=2 * high), :] = t[2 * resp : 2 * resp + 8]
         if count < high:
             res = res_ref[...]
             sq = jnp.broadcast_to(jnp.sum(res * res, axis=1, keepdims=True), (resp, LANES))
             for b in range(count, high):
                 for q in range(0, resp, 8):
                     part[p][pl.ds(q * high + b, 8, stride=high), :] = sq[q : q + 8]
-                gram[pl.ds(p * high + b, 8, stride=height), :] = jnp.zeros((8, LANES), jnp.float32)
-        if p == 0:
+                gram[p // 2][pl.ds(p % 2 * high + b, 8, stride=2 * high), :] = jnp.zeros(
+                    (8, LANES), jnp.float32
+                )
+        if p < hold:
+            continue
+        if p == hold:
             pl.semaphore_wait(barrier, peers)
-        else:
-            streams[p - 1].receive(0)
+        sent, flying = flying, []
+        for s in sent:
+            s.receive(0)
             if k > 1:
-                streams[p - 1].send(1)
-        streams[p].send(0)
-    grams.send(0)
+                s.send(1)
+        for i in range(p + 1) if p == hold else [p]:
+            flying.append(streams[i])
+            if i % 2:
+                flying.append(grams[i // 2])
+        for s in flying:
+            s.send(0)
 
     line, lane = place(multi_ref[...], basis)
     maps[...] = jnp.zeros_like(maps)
     maps[0:1, 0:cands] = line
     maps[1:2, 0:cands] = lane
-    for s in streams[parts - 1 :] + [grams]:
+    for s in flying:
         s.receive(0)
         if k > 1:
             s.send(1)
@@ -384,16 +409,23 @@
         one = jnp.where(row == at, 1.0, 0.0).astype(jnp.bfloat16)
         for i in range(3):
             hot[i * height : (i + 1) * height, c : c + LANES] = one
+    order = []
+    for p in range(parts):
+        order.append(streams[p])
+        if p % 2:
+            order.append(grams[p // 2])
     for stage in range(1, k):
-        for s in streams + [grams]:
+        for s in order:
             s.receive(stage)
             if stage + 1 < k:
                 s.send(stage + 1)
 
-    gplan, plan = grams.plan, streams[0].plan
+    gplan, plan = grams[0].plan, streams[0].plan
     at = pl.multiple_of(digit_place(ctx, gplan, digits) * unit, 8)
-    whole_gram[pl.ds(at, gplan[-1][1] * unit), :] = grams.now[...]
-    run_gram = spread(ctx, gplan, unit, whole_gram)
+    runs = []
+    for g in range(pieces):
+        whole_gram[g][pl.ds(at, gplan[-1][1] * unit), :] = grams[g].now[...]
+        runs.append(spread(ctx, gplan, unit, unit, whole_gram[g]))
 
     def arrange(row, store):
         first, rest = split(row)
@@ -412,24 +444,39 @@
                 store((c + i) // LANES, jnp.sum(kept, axis=0, keepdims=True))
 
     mine = digit_place(ctx, plan, digits) * height
-    for i in range(plan[-1][1]):
-        row = jnp.concatenate([s.now[i * high : (i + 1) * high, :] for s in streams], axis=0)
-        lines = [row[height - 1 :]] * (height - maps.shape[1] // LANES)
-        found = {}
-        arrange(row, found.__setitem__)
-        row = jnp.concatenate([found[b] for b in range(len(found))] + lines, axis=0)
-        total[pl.ds(pl.multiple_of(mine + i * height, 8), height), :] = row
-    run = spread(ctx, plan, height, total)
-    run_gram()
-    for g in range(iters):
-        row = whole_gram[g * height : (g + 1) * height, :]
+
+    def arranged(row):
         found = {}
         arrange(row, found.__setitem__)
         lines = [row[height - 1 :]] * (height - len(found))
-        out_ref[(resp + g) * height : (resp + g + 1) * height, :] = jnp.concatenate(
-            [found[b] for b in range(len(found))] + lines, axis=0
-        )
-    run()
+        return jnp.concatenate([found[b] for b in range(len(found))] + lines, axis=0)
+
+    for i in range(plan[-1][1]):
+        row = jnp.concatenate([s.now[i * high : (i + 1) * high, :] for s in streams], axis=0)
+        total[pl.ds(pl.multiple_of(mine + i * height, 8), height), :] = arranged(row)
+    run = spread(ctx, plan, height, up(maps.shape[1] // LANES + 1, tile), total)
+    last = [s for s, (cut, _) in enumerate(plan) if cut][-1]
+    todo = list(range(iters))
+
+    def gram_row():
+        if len(todo) == iters:
+            for r in runs:
+                for _ in r:
+                    pass
+        g = todo.pop(0)
+        span = slice(g * 2 * high, (g + 1) * 2 * high)
+        row = jnp.concatenate([w[span, :] for w in whole_gram], axis=0)
+        out_ref[(resp + g) * height : (resp + g + 1) * height, :] = arranged(row)
+
+    since = 0
+    for level in run:
+        if level == last:
+            continue
+        since += 1
+        if todo and since % 3 == 0:
+            gram_row()
+    while todo:
+        gram_row()
     rest = out_ref.shape[0] - (resp + iters) * height
     out_ref[(resp + iters) * height :, :] = jnp.zeros((rest, LANES), jnp.float32)
     out_ref[0 : resp * height, :] = total[...]
@@ -437,7 +484,7 @@
         c.wait_send()
 
 
-def finish(cands, samples, iters, height, chosen_ref, total_ref, res_ref, active_ref, out_ref, corr_ref, coef_ref, flat):
+def finish(cands, samples, iters, height, chosen_ref, total_ref, res_ref, active_ref, out_ref, corr_out, coef_ref, flat, corr_ref, sems):
     resp = res_ref.shape[0]
     for b in range(flat.shape[1] // LANES):
         for q in range(0, flat.shape[0], 8):
@@ -445,7 +492,10 @@
                 pl.ds(q * height + b, 8, stride=height), :
             ]
     sq = jnp.concatenate(
-        [total_ref[pl.ds(q * height + height - 1, 8, stride=height), :] for q in range(0, resp, 8)],
+        [
+            total_ref[pl.ds(q * height + flat.shape[1] // LANES, 8, stride=height), :]
+            for q in range(0, resp, 8)
+        ],
         axis=0,
     )[:, 0:1]
     total = flat[:, 0:cands]
@@ -466,9 +516,12 @@
     corr = total[0:resp]
     rows = [total[resp + i : resp + i + 1] for i in range(iters)]
     coef = [jnp.zeros((resp, 1), jnp.float32) for _ in range(iters)]
+    copies = []
     for k in range(iters):
         norm = math.sqrt(samples) * jnp.sqrt(sq / samples + 1e-06)
         corr_ref[k] = corr * (1.0 / norm)
+        copies.append(pltpu.make_async_copy(corr_ref.at[k], corr_out.at[k], sems.at[k]))
+        copies[-1].start()
         largest = jnp.max(jnp.abs(corr), axis=1, keepdims=True)
         gamma = jnp.abs(target[k]) / (largest + 1e-06)
         w = []
@@ -503,6 +556,8 @@
     lines = [jnp.sum(jnp.where(eye, c, 0.0), axis=0, keepdims=True) for c in coef]
     line = lax.broadcasted_iota(jnp.int32, coef_ref.shape, 0)
     coef_ref[...] = sum(jnp.where(line == i, lines[i], 0.0) for i in range(iters))
+    for c in copies:
+        c.wait()
 
 
 def on_device(inputs, response, multi_index, chosen):
@@ -521,13 +576,15 @@
     multi = multi_index.T
     vmem = pl.BlockSpec(memory_space=pltpu.VMEM)
     smem = pl.BlockSpec(memory_space=pltpu.SMEM)
-    deep = math.gcd(width, 512)
-    halves, parts = 2, 3
-    high, unit = height // parts, height // halves
+    hbm = pl.BlockSpec(memory_space=pltpu.HBM)
+    deep = width
+    halves, parts, tile = 2, 6, 4
+    high = height // parts
+    unit, pieces = 2 * high // halves, parts // 2
     stages = radices(devices)
     plan, gplan = halving(resp, stages), halving(kept * halves, stages)
-    copies = (parts + 1) * sum(r - 1 for r, _ in stages)
-    copies += resp // plan[-1][1] + kept * halves // gplan[-1][1] - 2
+    copies = (parts + pieces) * sum(r - 1 for r, _ in stages)
+    copies += resp // plan[-1][1] - 1 + pieces * (kept * halves // gplan[-1][1] - 1)
     grid = up(cands, LANES)
     lines = lambda n: pltpu.VMEM((n, LANES), jnp.float32)
     held = [lines(c * high) for _, c in plan]
@@ -535,8 +592,8 @@
     gheld = [lines(c * unit) for _, c in gplan]
     glanded = [lines(r * c * unit) for (r, _), (_, c) in zip(stages, gplan)]
     total, active = pl.pallas_call(
-        functools.partial(learn, basis, devices, parts, iters, deep, halves),
-        in_specs=[smem, vmem, vmem, vmem],
+        functools.partial(learn, basis, devices, parts, iters, deep, halves, tile),
+        in_specs=[smem, hbm, hbm, hbm],
         out_specs=[vmem, vmem],
         out_shape=[
             jax.ShapeDtypeStruct((used * height, LANES), jnp.float32),
@@ -545,20 +602,24 @@
         scratch_shapes=[
             pltpu.SemaphoreType.DMA((copies,)),
             pltpu.SemaphoreType.DMA((copies,)),
+            pltpu.SemaphoreType.DMA((3,)),
+            pltpu.VMEM(inputs.shape, jnp.float32),
+            pltpu.VMEM(response.shape, jnp.float32),
+            pltpu.VMEM(multi.shape, jnp.int32),
             pltpu.VMEM((3 * stride, width), jnp.float32),
             pltpu.VMEM((2 * nvars * stride, width), jnp.float32),
             pltpu.VMEM((up(2 * resp + few, LANES), width), jnp.bfloat16),
             lines(high * LANES),
             lines(resp * height),
-            lines(up(kept, 8) * height),
-            lines(kept * height),
             pltpu.VMEM((8, grid), jnp.float32),
             pltpu.VMEM((3 * height, grid), jnp.bfloat16),
             *[lines(resp * high) for _ in range(parts)],
             *(held * parts),
             *(landed * parts),
-            *gheld,
-            *glanded,
+            *[lines(up(kept, 8) * 2 * high) for _ in range(pieces)],
+            *[lines(kept * 2 * high) for _ in range(pieces)],
+            *(gheld * pieces),
+            *(glanded * pieces),
         ],
         compiler_params=pltpu.CompilerParams(
             vmem_limit_bytes=VMEM_LIMIT, collective_id=0, has_side_effects=True
@@ -568,13 +629,17 @@
     residual, corr, coef = pl.pallas_call(
         functools.partial(finish, cands, samples, iters, height),
         in_specs=[smem, vmem, vmem, vmem],
-        out_specs=[vmem, vmem, vmem],
+        out_specs=[vmem, pl.BlockSpec(memory_space=pl.ANY), vmem],
         out_shape=[
             jax.ShapeDtypeStruct((resp, width), jnp.float32),
             jax.ShapeDtypeStruct((iters, resp, cands), jnp.float32),
             jax.ShapeDtypeStruct((iters, resp), jnp.float32),
         ],
-        scratch_shapes=[pltpu.VMEM((used, grid), jnp.float32)],
+        scratch_shapes=[
+            pltpu.VMEM((used, grid), jnp.float32),
+            pltpu.VMEM((iters, resp, cands), jnp.float32),
+            pltpu.SemaphoreType.DMA((iters,)),
+        ],
         compiler_params=pltpu.CompilerParams(vmem_limit_bytes=VMEM_LIMIT),
         name="finish",
     )(chosen, total, response, active)

time: 44.5 us -> 41.7 us (0.937)
  Pallas kernels: 43.7 us -> 40.9 us
    pallas_call x1, Pallas kernels: 40 us -> 36.7 us  [on_device(): pl.pallas_call(functools.partial(learn, basis, devices, parts, iters, dee...]
    pallas_call x1, Pallas kernels: 3.69 us -> 4.21 us  [on_device(): pl.pallas_call(functools.partial(finish, cands, samples, iters, height),...]
where the time goes in v3:
time: 41.7 us; the launch traced here: 41.5 us
  Pallas kernels  40.9 us (98%)
  between operations  0.64 us (2%)
    pallas_call x1, Pallas kernels, on_device(): pl.pallas_call(functools.partial(learn, basis, devices, parts, iters, dee...  36.7 us
    pallas_call x1, Pallas kernels, on_device(): pl.pallas_call(functools.partial(finish, cands, samples, iters, height),...  4.21 us

profile of v3, /device:TPU:0, one launch (start us, length us, event | category | flops | bytes accessed | tf_op | source)
XLA Modules:
  0.0 41.5 jit_solution(18169176230386934474)
XLA Ops:
  0.6 36.7 %learn.1 = (f32[1920,128]{1,0:T(8,128)}, bf16[16,2048]{1,0:T(8,128)(2,1)}) custom-call(s32[3]{0:T(128)} %chosen_ref.3, f32[30,2048]{1,0:T(8,128)} %x_in.1, f32[32,2048]{1,0:T(8,128)} %res_ref.1, s32[30,5456]{1,0:T(8,128)} %bitcast.1), custom_call_target="tpu_custom_call" | custom-call | tf_op jit(solution)/shard_map/learn/pallas_call | solution.py:594
  37.3 4.2 %finish.1 = (f32[32,2048]{1,0:T(8,128)}, f32[3,32,5456]{2,1,0:T(8,128)}, f32[3,32]{1,0:T(4,128)}) custom-call(s32[3]{0:T(128)} %chosen_ref.3, f32[1920,128]{1,0:T(8,128)} %get-tuple-element.5.total_ref, f32[32,2048]{1,0:T(8,128)} %res_ref.1, bf16[16,2048]{1,0:T(8,128)(2,1)} %get-tuple-element.6.active_ref), custom_call_target="tpu_custom_call" | custom-call | tf_op jit(solution)/shard_map/finish/pallas_call | solution.py:629

commit v4 on v3

--- a/solution.py
+++ b/solution.py
@@ -199,6 +199,15 @@
     return result
 
 
+def partner(digit, j, r):
+    result, bit = 0, 1
+    while bit < r:
+        b = lax.rem(digit // bit, 2)
+        result = result + bit * (1 - b if j & bit else b)
+        bit *= 2
+    return result
+
+
 def halving(count, stages):
     plan = []
     for r, _ in stages:
@@ -242,7 +251,7 @@
         size = count * self.unit
         copies = []
         for j in range(r - 1, 0, -1):
-            other = lax.rem(digit + j, r)
+            other = partner(digit, j, r)
             peer = self.ctx["me"] + (other - digit) * stride
             at = pl.multiple_of(other * size, 8) if cut else 0
             copies.append(
@@ -270,7 +279,7 @@
             landed[0:size, :] = own
             total = None
             for i in range(r):
-                at = pl.multiple_of(lax.rem(digit + r - i, r) * size, 8)
+                at = pl.multiple_of(partner(digit, i, r) * size, 8)
                 term = landed[pl.ds(at, size), :]
                 total = term if total is None else total + term
         self.held[s][...] = total
@@ -297,12 +306,14 @@
         for s in reversed(below):
             r, stride = ctx["stages"][s]
             digit = ctx["digits"][s]
+            arrivals = []
             for j in range(r - 1, 0, -1):
-                peer = ctx["me"] + (lax.rem(digit + j, r) - digit) * stride
+                peer = ctx["me"] + (partner(digit, j, r) - digit) * stride
                 c = ctx["sems"].copy(block, block, peer)
                 source = dict(digits)
-                source[s] = lax.rem(digit + r - j, r)
-                arriving[s].append((c, source))
+                source[s] = partner(digit, j, r)
+                arrivals.insert(0, (c, source))
+            arriving[s] += arrivals
 
     forward(dict(enumerate(ctx["digits"])), levels)
 
@@ -344,7 +355,7 @@
     peers = 0
     for (r, stride), digit in zip(stages, digits):
         for j in range(1, r):
-            peer = me + (lax.rem(digit + j, r) - digit) * stride
+            peer = me + (partner(digit, j, r) - digit) * stride
             pl.semaphore_signal(barrier, inc=1, device_id=(peer,), device_id_type=MESH)
             peers += 1
 
@@ -399,26 +410,31 @@
     maps[...] = jnp.zeros_like(maps)
     maps[0:1, 0:cands] = line
     maps[1:2, 0:cands] = lane
+    def advance(s, stage):
+        s.receive(stage)
+        if stage + 1 < k:
+            s.send(stage + 1)
+
+    order = []
+    for p in range(parts):
+        order.append(streams[p])
+        if p % 2:
+            order.append(grams[p // 2])
+    early = order[: len(order) // 2] if k > 1 else []
+    for s in early:
+        advance(s, 1)
     for s in flying:
-        s.receive(0)
-        if k > 1:
-            s.send(1)
+        advance(s, 0)
     for c in range(0, maps.shape[1], LANES):
         at = maps[0:1, c : c + LANES]
         row = lax.broadcasted_iota(jnp.int32, (height, LANES), 0).astype(jnp.float32)
         one = jnp.where(row == at, 1.0, 0.0).astype(jnp.bfloat16)
         for i in range(3):
             hot[i * height : (i + 1) * height, c : c + LANES] = one
-    order = []
-    for p in range(parts):
-        order.append(streams[p])
-        if p % 2:
-            order.append(grams[p // 2])
     for stage in range(1, k):
         for s in order:
-            s.receive(stage)
-            if stage + 1 < k:
-                s.send(stage + 1)
+            if stage > 1 or s not in early:
+                advance(s, stage)
 
     gplan, plan = grams[0].plan, streams[0].plan
     at = pl.multiple_of(digit_place(ctx, gplan, digits) * unit, 8)

time: 41.7 us -> 41.5 us (level)
  no operation moved by 1% of the time
where the time goes in v4:
time: 41.5 us; the launch traced here: 41.3 us
  Pallas kernels  40.7 us (98%)
  between operations  0.64 us (2%)
    pallas_call x1, Pallas kernels, on_device(): pl.pallas_call(functools.partial(learn, basis, devices, parts, iters, dee...  36.5 us
    pallas_call x1, Pallas kernels, on_device(): pl.pallas_call(functools.partial(finish, cands, samples, iters, height),...  4.21 us

profile of v4, /device:TPU:0, one launch (start us, length us, event | category | flops | bytes accessed | tf_op | source)
XLA Modules:
  0.0 41.3 jit_solution(7111962573794784641)
XLA Ops:
  0.6 36.5 %learn.1 = (f32[1920,128]{1,0:T(8,128)}, bf16[16,2048]{1,0:T(8,128)(2,1)}) custom-call(s32[3]{0:T(128)} %chosen_ref.3, f32[30,2048]{1,0:T(8,128)} %x_in.1, f32[32,2048]{1,0:T(8,128)} %res_ref.1, s32[30,5456]{1,0:T(8,128)} %bitcast.1), custom_call_target="tpu_custom_call" | custom-call | tf_op jit(solution)/shard_map/learn/pallas_call | solution.py:610
  37.1 4.2 %finish.1 = (f32[32,2048]{1,0:T(8,128)}, f32[3,32,5456]{2,1,0:T(8,128)}, f32[3,32]{1,0:T(4,128)}) custom-call(s32[3]{0:T(128)} %chosen_ref.3, f32[1920,128]{1,0:T(8,128)} %get-tuple-element.5.total_ref, f32[32,2048]{1,0:T(8,128)} %res_ref.1, bf16[16,2048]{1,0:T(8,128)(2,1)} %get-tuple-element.6.active_ref), custom_call_target="tpu_custom_call" | custom-call | tf_op jit(solution)/shard_map/finish/pallas_call | solution.py:645

commit v5 on v4

--- a/solution.py
+++ b/solution.py
@@ -322,7 +322,7 @@
             for c, digits in arriving[levels[i]]:
                 c.wait_recv()
                 forward(digits, levels[:i])
-                yield levels[i]
+                yield levels[i], digits
 
     return run()
 
@@ -335,8 +335,8 @@
     stages = radices(devices)
     me = lax.axis_index("samp")
     digits = [lax.rem(me // stride, r) for r, stride in stages]
-    send, recv, loaded, x_ref, res_ref, multi_ref, twice, turned, rows, acc, total, maps, hot = scratch[:13]
-    buffers = scratch[13:]
+    send, recv, loaded, stored, extra, x_ref, res_ref, multi_ref, twice, turned, rows, acc, total, maps, hot = scratch[:15]
+    buffers = scratch[15:]
     loads = []
     for i, (a, b) in enumerate([(x_in, x_ref), (multi_in, multi_ref), (res_in, res_ref)]):
         loads.append(pltpu.make_async_copy(a, b, loaded.at[i]))
@@ -472,6 +472,24 @@
         total[pl.ds(pl.multiple_of(mine + i * height, 8), height), :] = arranged(row)
     run = spread(ctx, plan, height, up(maps.shape[1] // LANES + 1, tile), total)
     last = [s for s, (cut, _) in enumerate(plan) if cut][-1]
+    size = (plan[-1][1] - 1) * height + up(maps.shape[1] // LANES + 1, tile)
+    stores = []
+
+    def store(src, dst):
+        stores.append(pltpu.make_async_copy(src, dst, stored.at[len(stores)]))
+        stores[-1].start()
+
+    def keep(source):
+        at = pl.multiple_of(digit_place(ctx, plan, source) * height, 8)
+        store(total.at[pl.ds(at, size)], out_ref.at[pl.ds(at, size)])
+
+    keep(dict(enumerate(digits)))
+    rest = extra.shape[0] - iters * height
+    extra[iters * height :, :] = jnp.zeros((rest, LANES), jnp.float32)
+    store(
+        extra.at[pl.ds(iters * height, rest)],
+        out_ref.at[pl.ds((resp + iters) * height, rest)],
+    )
     todo = list(range(iters))
 
     def gram_row():
@@ -482,10 +500,15 @@
         g = todo.pop(0)
         span = slice(g * 2 * high, (g + 1) * 2 * high)
         row = jnp.concatenate([w[span, :] for w in whole_gram], axis=0)
-        out_ref[(resp + g) * height : (resp + g + 1) * height, :] = arranged(row)
+        extra[g * height : (g + 1) * height, :] = arranged(row)
+        store(
+            extra.at[pl.ds(g * height, height)],
+            out_ref.at[pl.ds((resp + g) * height, height)],
+        )
 
     since = 0
-    for level in run:
+    for level, source in run:
+        keep(source)
         if level == last:
             continue
         since += 1
@@ -493,9 +516,8 @@
             gram_row()
     while todo:
         gram_row()
-    rest = out_ref.shape[0] - (resp + iters) * height
-    out_ref[(resp + iters) * height :, :] = jnp.zeros((rest, LANES), jnp.float32)
-    out_ref[0 : resp * height, :] = total[...]
+    for c in stores:
+        c.wait()
     for c in ctx["sems"].sent:
         c.wait_send()
 
@@ -610,7 +632,7 @@
     total, active = pl.pallas_call(
         functools.partial(learn, basis, devices, parts, iters, deep, halves, tile),
         in_specs=[smem, hbm, hbm, hbm],
-        out_specs=[vmem, vmem],
+        out_specs=[hbm, vmem],
         out_shape=[
             jax.ShapeDtypeStruct((used * height, LANES), jnp.float32),
             jax.ShapeDtypeStruct((few, width), jnp.bfloat16),
@@ -619,6 +641,8 @@
             pltpu.SemaphoreType.DMA((copies,)),
             pltpu.SemaphoreType.DMA((copies,)),
             pltpu.SemaphoreType.DMA((3,)),
+            pltpu.SemaphoreType.DMA((resp // plan[-1][1] + iters + 1,)),
+            lines(extra * height),
             pltpu.VMEM(inputs.shape, jnp.float32),
             pltpu.VMEM(response.shape, jnp.float32),
             pltpu.VMEM(multi.shape, jnp.int32),

time: 41.5 us -> 41.9 us (level)
    pallas_call x1, Pallas kernels: 36.5 us -> 36.9 us  [on_device(): pl.pallas_call(functools.partial(learn, basis, devices, parts, iters, dee...]
where the time goes in v5:
time: 41.9 us; the launch traced here: 41.8 us
  Pallas kernels  41.1 us (98%)
  between operations  0.64 us (2%)
    pallas_call x1, Pallas kernels, on_device(): pl.pallas_call(functools.partial(learn, basis, devices, parts, iters, dee...  36.9 us
    pallas_call x1, Pallas kernels, on_device(): pl.pallas_call(functools.partial(finish, cands, samples, iters, height),...  4.21 us

profile of v5, /device:TPU:0, one launch (start us, length us, event | category | flops | bytes accessed | tf_op | source)
XLA Modules:
  0.0 41.8 jit_solution(11291425724986801416)
XLA Ops:
  0.6 36.9 %learn.1 = (f32[1920,128]{1,0:T(8,128)}, bf16[16,2048]{1,0:T(8,128)(2,1)}) custom-call(s32[3]{0:T(128)} %chosen_ref.3, f32[30,2048]{1,0:T(8,128)} %x_in.1, f32[32,2048]{1,0:T(8,128)} %res_ref.1, s32[30,5456]{1,0:T(8,128)} %bitcast.1), custom_call_target="tpu_custom_call" | custom-call | tf_op jit(solution)/shard_map/learn/pallas_call | solution.py:632
  37.6 4.2 %finish.1 = (f32[32,2048]{1,0:T(8,128)}, f32[3,32,5456]{2,1,0:T(8,128)}, f32[3,32]{1,0:T(4,128)}) custom-call(s32[3]{0:T(128)} %chosen_ref.3, f32[1920,128]{1,0:T(8,128)} %get-tuple-element.5.total_ref, f32[32,2048]{1,0:T(8,128)} %res_ref.1, bf16[16,2048]{1,0:T(8,128)(2,1)} %get-tuple-element.6.active_ref), custom_call_target="tpu_custom_call" | custom-call | tf_op jit(solution)/shard_map/finish/pallas_call | solution.py:669
